TPU v7x, 128 devices: a whole 4x4x4 slice. The times are simulated.
128 devices in a mesh: dp: 1, ty: 16 (over z, y), tx: 8 (over x, core).
Axes of the slice: x: 4, y: 4, z: 4, core: 2. Of those that a mesh axis runs over, the one named last changes fastest.
Arguments:
- x_in: bfloat16 [16, 512, 4096], P(('dp', 'ty'), None, 'tx')
- w_q: bfloat16 [4096, 4096], P('tx', 'ty')
- w_k: bfloat16 [4096, 4096], P('tx', 'ty')
- w_v: bfloat16 [4096, 4096], P('tx', 'ty')
- w_o: bfloat16 [4096, 4096], P('ty', 'tx')
- w_gate: bfloat16 [4096, 11008], P('tx', 'ty')
- w_up: bfloat16 [4096, 11008], P('tx', 'ty')
- w_down: bfloat16 [11008, 4096], P('ty', 'tx')
Outputs:
- output: bfloat16 [16, 512, 4096], P(('dp', 'ty'), None, 'tx')
All inputs are finite; a program needn't handle non-finite values.
Results may differ from a plain program's by a relative error of at most 0.02.
Values are sent between devices in bfloat16 or wider.
A program may use at most 1 GiB of HBM per device.

v0:
```python
import jax
import jax.numpy as jnp
from jax import lax
from jax.sharding import PartitionSpec as P, NamedSharding

HEAD_DIM = 128
EPS = 1e-5
THETA = 10000.0


def rotary(heads_bf):
    seq_len = heads_bf.shape[1]
    half_dim = HEAD_DIM // 2
    inv_freq = THETA ** (-2.0 * jnp.arange(half_dim, dtype=jnp.float32) / HEAD_DIM)
    angles = jnp.arange(seq_len, dtype=jnp.float32)[:, None] * inv_freq[None, :]
    cos_t = jnp.cos(angles)[:, None, :]
    sin_t = jnp.sin(angles)[:, None, :]
    values = heads_bf.astype(jnp.float32)
    lower_half = values[..., :half_dim]
    upper_half = values[..., half_dim:]
    return jnp.concatenate([lower_half * cos_t - upper_half * sin_t, upper_half * cos_t + lower_half * sin_t], axis=-1).astype(jnp.bfloat16)


def causal_attention(q_heads, k_heads, v_heads):
    seq_len = q_heads.shape[1]
    q_block = min(seq_len, 128)
    key_pos = jnp.arange(seq_len)
    scale_qk = HEAD_DIM ** -0.5

    def one_block(block_idx, out_acc):
        q_start = block_idx * q_block
        q_blk = lax.dynamic_slice_in_dim(q_heads, q_start, q_block, axis=1)
        scores = jnp.einsum("nqhd,nkhd->nhqk", q_blk, k_heads, preferred_element_type=jnp.float32) * scale_qk
        q_pos = q_start + jnp.arange(q_block)
        allowed = q_pos[:, None] >= key_pos[None, :]
        scores = jnp.where(allowed, scores, -1e30)
        prob_blk = jax.nn.softmax(scores, axis=-1).astype(jnp.bfloat16)
        blk_out = jnp.einsum("nhqk,nkhd->nqhd", prob_blk, v_heads, preferred_element_type=jnp.float32).astype(jnp.bfloat16)
        return lax.dynamic_update_slice_in_dim(out_acc, blk_out, q_start, axis=1)

    return lax.fori_loop(0, seq_len // q_block, one_block, jnp.zeros_like(q_heads))


def norm_sharded(values_bf, full_width):
    values = values_bf.astype(jnp.float32)
    moments = jnp.stack([jnp.sum(values, axis=-1), jnp.sum(values * values, axis=-1)], axis=-1)
    moments = lax.psum(moments, "tx")
    mean_val = moments[..., 0:1] / full_width
    var_val = moments[..., 1:2] / full_width - mean_val * mean_val
    return ((values - mean_val) * lax.rsqrt(var_val + EPS)).astype(jnp.bfloat16)


def project(rows_bf, weight):
    return jnp.einsum("...c,ch->...h", rows_bf, weight, preferred_element_type=jnp.float32).astype(jnp.bfloat16)


def solution(mesh):
    tx_count = mesh.shape["tx"]
    act_spec = P(("dp", "ty"), None, "tx")
    col_spec = P("tx", "ty")
    row_spec = P("ty", "tx")

    def layer_fn(x_blk, w_q, w_k, w_v, w_o, w_gate, w_up, w_down):
        full_width = x_blk.shape[-1] * tx_count
        normed_all = lax.all_gather(norm_sharded(x_blk, full_width), "ty", axis=0, tiled=True)
        q_sum, k_sum, v_sum = lax.psum((project(normed_all, w_q), project(normed_all, w_k), project(normed_all, w_v)), "tx")
        n_seqs, seq_len, local_cols = q_sum.shape
        head_shape = (n_seqs, seq_len, local_cols // HEAD_DIM, HEAD_DIM)
        attn_heads = causal_attention(rotary(q_sum.reshape(head_shape)), rotary(k_sum.reshape(head_shape)), v_sum.reshape(head_shape))
        attn_out = lax.psum_scatter(project(attn_heads.reshape(q_sum.shape), w_o), "ty", scatter_dimension=0, tiled=True)
        resid_h = (x_blk.astype(jnp.float32) + attn_out.astype(jnp.float32)).astype(jnp.bfloat16)
        normed_mlp = lax.all_gather(norm_sharded(resid_h, full_width), "ty", axis=0, tiled=True)
        gate_sum, up_sum = lax.psum((project(normed_mlp, w_gate), project(normed_mlp, w_up)), "tx")
        act_val = (jax.nn.silu(gate_sum.astype(jnp.float32)) * up_sum.astype(jnp.float32)).astype(jnp.bfloat16)
        mlp_out = lax.psum_scatter(project(act_val, w_down), "ty", scatter_dimension=0, tiled=True)
        return (resid_h.astype(jnp.float32) + mlp_out.astype(jnp.float32)).astype(jnp.bfloat16)

    return jax.shard_map(layer_fn, mesh=mesh, in_specs=(act_spec, col_spec, col_spec, col_spec, row_spec, col_spec, col_spec, row_spec), out_specs=act_spec, check_vma=False)
```

profile of v0, /device:TPU:1, one launch (start us, length us, event | category | flops | bytes accessed | tf_op | source)
XLA Modules:
  0.0 933.0 jit_solution(144450095563361680)
XLA Ops:
  6.5 1.4 convert_reduce_fusion.1
  7.9 13.2 %psum.49 = f32[1,512,2]{1,2,0:T(2,128)S(1)} all-reduce(f32[1,512,2]{1,2,0:T(2,128)S(1)} %pad_maximum_fusion.2), channel_id=1, replica_groups=mesh['dp'=1,'ty'=16,'tx'=8] {'tx'}, use_global_device_ids=true, to_apply=%region_2.0 | all-reduce | flops 1024 | bytes 8192 | tf_op jit(solution)/shard_map/psum | solution.py:47
  21.1 2.0 fusion.27
  23.2 0.0 all-gather.3.cloned.1.call-update
  23.2 0.0 all-reduce.9.cloned.1.call-start
  23.3 72.7 %all-gather.3.cloned.1.call-done = bf16[16,512,512]{2,1,0:T(8,128)(2,1)} async-done(((bf16[1,512,512]{2,1,0:T(8,128)(2,1)}), bf16[16,512,512]{2,1,0:T(8,128)(2,1)}) %all-gather.3.cloned.1.call-update) | async-done | bytes 8388624 | tf_op jit(solution)/shard_map/all_gather | solution.py:65
  96.0 7.7 convolution_convert_fusion.3
  103.7 6.4 copy.28
  110.1 7.7 convolution_convert_fusion.5
  117.8 6.4 copy.24
  124.2 7.7 convolution_convert_fusion.4
  131.9 6.4 copy.26
  138.3 0.0 all-reduce.9.cloned.1.call-update
  138.3 0.0 reduce-scatter.7.cloned.1.call-start
  138.4 1.0 fusion.41
  139.3 142.4 %all-reduce.9.cloned.1.call-done = (bf16[16,512,2,128]{3,1,2,0:T(8,128)(2,1)}, bf16[16,512,2,128]{3,1,2,0:T(8,128)(2,1)}, bf16[16,512,2,128]{3,1,2,0:T(8,128)(2,1)}) async-done(((bf16[16,512,2,128]{3,1,2,0:T(8,128)(2,1)}, bf16[16,512,2,128]{3,1,2,0:T(8,128)(2,1)}, bf16[16,512,2,128]{3,1,2,0:T(8,128)(2,1)}), (bf16[16,512,2,128]{3,1,2,0:T(8,128)(2,1)}, bf16[16,512,2,128]{3,1,2,0:T(8,128)(2,1)}, ...) | async-done | bytes 12582928 | tf_op jit(solution)/shard_map/psum | solution.py:66
  281.7 6.6 convert_element_type.91
  288.3 4.2 convert_element_type.94
  292.5 19.0 %subtract_convert_fusion = (bf16[16,512,2,64]{3,1,2,0:T(8,128)(2,1)}, bf16[16,512,2,64]{3,1,2,0:T(8,128)(2,1)}, bf16[16,512,2,64]{3,1,2,0:T(8,128)(2,1)}, bf16[16,512,2,64]{3,1,2,0:T(8,128)(2,1)}) fusion(f32[16,512,2,128]{3,1,2,0:T(8,128)} %convert_element_type.94, f32[512,64]{1,0:T(8,128)S(1)} %get-tuple-element.160, f32[512,64]{1,0:T(8,128)S(1)} %get-tuple-element.159, ...), kind=kLoop, calls=%fused_computation.29 | loop fusion | flops 16777216 | bytes 25427968 | tf_op jit(solution)/shard_map/convert.2
  311.5 10.1 %pad_maximum_fusion = (bf16[16,512,2,128]{3,1,2,0:T(8,128)(2,1)}, bf16[16,512,2,128]{3,1,2,0:T(8,128)(2,1)}) fusion(bf16[16,512,2,64]{3,1,2,0:T(8,128)(2,1)} %get-tuple-element.153, bf16[16,512,2,64]{3,1,2,0:T(8,128)(2,1)} %get-tuple-element.154, bf16[16,512,2,64]{3,1,2,0:T(8,128)(2,1)} %get-tuple-element.150, bf16[16,512,2,64]{3,1,2,0:T(8,128)(2,1)} %get-tuple-element.149), kind=kLoop, calls=%fused_computation.36 | loop fusion | flops 16777216 | bytes 16777216 | tf_op jit(solution)/shard_map/concatenate | solution.py:21
  321.6 2.4 broadcast_in_dim.35.clone
  324.0 65.7 %while.14 = (s32[]{:T(128)}, bf16[16,512,2,128]{1,3,2,0:T(8,128)(2,1)}, bf16[16,512,2,128]{3,1,2,0:T(8,128)(2,1)}, bf16[16,512,2,128]{3,1,2,0:T(8,128)(2,1)}, bf...) while((s32[]{:T(128)}, ...), condition=%wide.region_9.10_spmd.clone, body=%wide.region_6.9_spmd.clone.sunk | while | flops 1091109504 | bytes 65176752 | solution.py:41
  324.0 0.1 iota_compare_fusion.2
  324.2 3.8 fusion.64
  327.9 6.0 fusion.65
  333.9 4.7 fusion.66
  338.7 0.7 copy.41
  339.3 1.1 constant_dynamic-update-slice_fusion.2
  340.4 0.1 iota_compare_fusion.2
  340.5 3.8 fusion.64
  344.3 6.0 fusion.65
  350.3 4.7 fusion.66
  355.0 0.7 copy.41
  355.7 1.1 constant_dynamic-update-slice_fusion.2
  356.8 0.1 iota_compare_fusion.2
  356.9 3.8 fusion.64
  360.7 6.0 fusion.65
  366.7 4.7 fusion.66
  371.5 0.7 copy.41
  372.1 1.2 constant_dynamic-update-slice_fusion.2
  373.3 0.1 iota_compare_fusion.2
  373.4 3.8 fusion.64
  377.2 6.0 fusion.65
  383.2 4.7 fusion.66
  387.9 0.7 copy.41
  388.6 1.2 constant_dynamic-update-slice_fusion.2
  389.8 7.9 convolution_convert_fusion.2
  397.6 0.0 reduce-scatter.7.cloned.1.call-update
  397.7 0.0 all-gather.5.cloned.1.call-start
  397.7 84.1 %reduce-scatter.7.cloned.1.call-done = bf16[1,512,512]{2,1,0:T(8,128)(2,1)} async-done(((bf16[16,512,512]{2,1,0:T(8,128)(2,1)}), bf16[1,512,512]{2,1,0:T(8,128)(2,1)}) %reduce-scatter.7.cloned.1.call-update) | async-done | bytes 524304
  481.8 1.3 convert_reduce_fusion
  483.1 14.2 %psum.53 = f32[1,512,2]{1,2,0:T(2,128)S(1)} all-reduce(f32[1,512,2]{1,2,0:T(2,128)S(1)} %pad_maximum_fusion.3), channel_id=1, replica_groups=mesh['dp'=1,'ty'=16,'tx'=8] {'tx'}, use_global_device_ids=true, to_apply=%region_13.14 | all-reduce | flops 1024 | bytes 8192 | tf_op jit(solution)/shard_map/psum | solution.py:47
  497.3 1.0 fusion.31
  498.3 0.0 all-gather.5.cloned.1.call-update
  498.3 0.0 all-reduce.7.cloned.1.call-start
  498.4 67.8 %all-gather.5.cloned.1.call-done = bf16[16,512,512]{2,1,0:T(8,128)(2,1)} async-done(((bf16[1,512,512]{2,1,0:T(8,128)(2,1)}), bf16[16,512,512]{2,1,0:T(8,128)(2,1)}) %all-gather.5.cloned.1.call-update) | async-done | bytes 8388624 | tf_op jit(solution)/shard_map/all_gather | solution.py:72
  566.2 12.2 %convolution_convert_fusion = bf16[16,512,688]{1,2,0:T(8,128)(2,1)} fusion(bf16[16,512,512]{2,1,0:T(8,128)(2,1)} %all-gather.5.cloned.1.call-done, bf16[512,688]{0,1:T(8,128)(2,1)S(1)} %copy-done), kind=kOutput, calls=%fused_computation.32 | convolution fusion | flops 5776998400 | bytes 20365312 | tf_op jit(solution)/shard_map/...c,ch->...h/dot_general | solution.py:54
  578.5 8.9 convolution_convert_fusion.1
  587.4 0.0 all-reduce.7.cloned.1.call-update
  587.4 0.0 reduce-scatter.9.cloned.1.call-start
  587.4 236.6 %all-reduce.7.cloned.1.call-done = (bf16[16,512,688]{1,2,0:T(8,128)(2,1)}, bf16[16,512,688]{1,2,0:T(8,128)(2,1)}) async-done(((bf16[16,512,688]{1,2,0:T(8,128)(2,1)}, bf16[16,512,688]{1,2,0:T(8,128)(2,1)}), (bf16[16,512,688]{1,2,0:T(8,128)(2,1)}, bf16[16,512,688]{1,2,0:T(8,128)(2,1)})) %all-reduce.7.cloned.1.call-update) | async-done | bytes 22544400 | tf_op jit(solution)/shard_map/psum | solution.py:73
  824.0 15.9 %fusion.22 = bf16[16,512,512]{2,1,0:T(8,128)(2,1)} fusion(bf16[16,512,688]{1,2,0:T(8,128)(2,1)} %get-tuple-element.141, bf16[16,512,688]{1,2,0:T(8,128)(2,1)} %get-tuple-element.142, bf16[688,512]{1,0:T(8,128)(2,1)S(1)} %copy-done.9), kind=kOutput, calls=%fused_computation.35 | convolution fusion | flops 5820645376 | bytes 31637504 | tf_op jit(solution)/shard_map/...c,ch->...h/dot_general | solution.py:54
  840.0 84.2 %reduce-scatter.9.cloned.1.call-done = bf16[1,512,512]{2,1,0:T(8,128)(2,1)} async-done(((bf16[16,512,512]{2,1,0:T(8,128)(2,1)}), bf16[1,512,512]{2,1,0:T(8,128)(2,1)}) %reduce-scatter.9.cloned.1.call-update) | async-done | bytes 524304
  924.2 2.0 fusion.32
  (37 shorter events, 0.1 us)
Async XLA Ops:
  6.5 559.7 %copy-start = (bf16[512,688]{0,1:T(8,128)(2,1)S(1)}, bf16[512,688]{0,1:T(8,128)(2,1)}, u32[]{:S(2)}) copy-start(bf16[512,688]{0,1:T(8,128)(2,1)} %param.16) | copy-start | bytes 2113540
  6.5 89.4 %all-gather.3.cloned.1.call-start = ((), (), s32[]{:S(2)}) async-start(), calls=%async_computation.2 | async-start | bytes 8912896 | tf_op jit(solution)/shard_map/all_gather | solution.py:65
  23.2 86.9 %copy-start.3 = (bf16[512,256]{1,0:T(8,128)(2,1)S(1)}, bf16[512,256]{1,0:T(8,128)(2,1)}, u32[]{:S(2)}) copy-start(bf16[512,256]{1,0:T(8,128)(2,1)} %param.11) | copy-start | bytes 786436
  23.2 258.5 %all-reduce.9.cloned.1.call-start = ((), (), s32[]{:S(2)}) async-start(), calls=%async_computation.7 | async-start | bytes 25165824 | tf_op jit(solution)/shard_map/psum | solution.py:66
  110.1 14.1 %copy-start.4 = (bf16[512,256]{1,0:T(8,128)(2,1)S(1)}, bf16[512,256]{1,0:T(8,128)(2,1)}, u32[]{:S(2)}) copy-start(bf16[512,256]{1,0:T(8,128)(2,1)} %param.12) | copy-start | bytes 786436
  138.3 343.5 %reduce-scatter.7.cloned.1.call-start = ((), (), s32[]{:S(2)}) async-start(), calls=%async_computation.4 | async-start | bytes 8912896
  281.7 6.6 copy-start.2
  324.0 65.7 %copy-start.5 = (bf16[256,512]{1,0:T(8,128)(2,1)S(1)}, bf16[256,512]{1,0:T(8,128)(2,1)}, u32[]{:S(2)}) copy-start(bf16[256,512]{1,0:T(8,128)(2,1)} %param.14) | copy-start | bytes 786436
  327.9 6.0 copy-start.7
  344.3 6.0 copy-start.7
  360.7 6.0 copy-start.7
  377.2 6.0 copy-start.7
  389.8 92.0 %copy-start.1 = (bf16[1,512,512]{2,1,0:T(8,128)(2,1)S(1)}, bf16[1,512,512]{2,1,0:T(8,128)(2,1)}, u32[]{:S(2)}) copy-start(bf16[1,512,512]{2,1,0:T(8,128)(2,1)} %param.10) | copy-start | bytes 1572868
  397.7 168.5 %all-gather.5.cloned.1.call-start = ((), (), s32[]{:S(2)}) async-start(), calls=%async_computation.3 | async-start | bytes 8912896 | tf_op jit(solution)/shard_map/all_gather | solution.py:72
  498.3 80.1 %copy-start.8 = (bf16[512,688]{0,1:T(8,128)(2,1)S(1)}, bf16[512,688]{0,1:T(8,128)(2,1)}, u32[]{:S(2)}) copy-start(bf16[512,688]{0,1:T(8,128)(2,1)} %param.15) | copy-start | bytes 2113540
  498.3 325.7 %all-reduce.7.cloned.1.call-start = ((), (), s32[]{:S(2)}) async-start(), calls=%async_computation.6 | async-start | bytes 45088768 | tf_op jit(solution)/shard_map/psum | solution.py:73
  566.2 12.2 %copy-start.6 = (bf16[16,512,512]{2,1,0:T(8,128)(2,1)S(1)}, bf16[16,512,512]{2,1,0:T(8,128)(2,1)}, u32[]{:S(2)}) copy-start(bf16[16,512,512]{2,1,0:T(8,128)(2,1)} %all-gather.5.cloned.1.call-done) | copy-start | bytes 25165828
  587.4 236.6 %copy-start.9 = (bf16[688,512]{1,0:T(8,128)(2,1)S(1)}, bf16[688,512]{1,0:T(8,128)(2,1)}, u32[]{:S(2)}) copy-start(bf16[688,512]{1,0:T(8,128)(2,1)} %param.17) | copy-start | bytes 2113540
  587.4 336.8 %reduce-scatter.9.cloned.1.call-start = ((), (), s32[]{:S(2)}) async-start(), calls=%async_computation.5 | async-start | bytes 8912896
Sparse Core Ops, SparseCore 0:
  23.3 72.6 all-gather.2
  138.4 143.2 all-reduce.8
  397.8 83.9 reduce-scatter.6
  498.5 67.7 all-gather.4
  587.5 236.4 all-reduce.6
  840.1 84.0 reduce-scatter.8
where the time goes:
time: 935 us; the launch traced here: 933 us
  waiting for transfers between devices  688 us (74%)
  matrix products  102 us (11%)
  other arithmetic  72.9 us (8%)
  local copies, waits for them, and re-layouts  28.8 us (3%)
  blocking collectives  27.4 us (3%)
  between operations  13.5 us (1%)
    psum x1, waiting for transfers between devices, layer_fn(): lax.psum((project(normed_mlp, w_gate), project(normed_mlp, w_up)), 'tx')  237 us
    unnamed x8, waiting for transfers between devices  168 us
    psum x1, waiting for transfers between devices, layer_fn(): lax.psum((project(normed_all, w_q), project(normed_all, w_k), project(nor...  142 us
    all_gather x1, waiting for transfers between devices, layer_fn(): lax.all_gather(norm_sharded(x_blk, full_width), 'ty', axis=0, tiled=True)  72.7 us
    dot_general x7, matrix products, project(): jnp.einsum('...c,ch->...h', rows_bf, weight, preferred_element_type=jnp.f...  68.1 us
    all_gather x1, waiting for transfers between devices, layer_fn(): lax.all_gather(norm_sharded(resid_h, full_width), 'ty', axis=0, tiled=True)  67.8 us
    psum x2, blocking collectives, norm_sharded(): moments = lax.psum(moments, 'tx')  27.4 us
    sub x4, other arithmetic, one_block(): prob_blk = jax.nn.softmax(scores, axis=-1).astype(jnp.bfloat16)  23.8 us
  transfers between devices with their start and end apart: 6, of which 6 were waited for; matrix products, arithmetic and copies ran while one was open for 0% of the time, Pallas kernels for 0%

commit v1 on v0

v1 whole, which is shorter than its diff:
```python
import jax
import jax.numpy as jnp
from jax import lax
from jax.sharding import PartitionSpec as P

HEAD_DIM = 128
EPS = 1e-5
THETA = 10000.0


def rotary(heads_bf):
    seq_len = heads_bf.shape[1]
    half_dim = HEAD_DIM // 2
    inv_freq = THETA ** (-2.0 * jnp.arange(half_dim, dtype=jnp.float32) / HEAD_DIM)
    angles = jnp.arange(seq_len, dtype=jnp.float32)[:, None] * inv_freq[None, :]
    cos_t = jnp.cos(angles)[:, None, :]
    sin_t = jnp.sin(angles)[:, None, :]
    values = heads_bf.astype(jnp.float32)
    lower_half = values[..., :half_dim]
    upper_half = values[..., half_dim:]
    return jnp.concatenate([lower_half * cos_t - upper_half * sin_t, upper_half * cos_t + lower_half * sin_t], axis=-1).astype(jnp.bfloat16)


def causal_attention(q_heads, k_heads, v_heads):
    seq_len = q_heads.shape[1]
    pos = jnp.arange(seq_len)
    scores = jnp.einsum("nqhd,nkhd->nhqk", q_heads, k_heads, preferred_element_type=jnp.float32) * HEAD_DIM ** -0.5
    scores = jnp.where(pos[:, None] >= pos[None, :], scores, -1e30)
    prob = jax.nn.softmax(scores, axis=-1).astype(jnp.bfloat16)
    return jnp.einsum("nhqk,nkhd->nqhd", prob, v_heads, preferred_element_type=jnp.float32).astype(jnp.bfloat16)


def norm_full(values_bf):
    values = values_bf.astype(jnp.float32)
    mean_val = jnp.mean(values, axis=-1, keepdims=True)
    var_val = jnp.mean(values * values, axis=-1, keepdims=True) - mean_val * mean_val
    return ((values - mean_val) * lax.rsqrt(var_val + EPS)).astype(jnp.bfloat16)


def project(rows_bf, weight):
    return jnp.einsum("...c,ch->...h", rows_bf, weight, preferred_element_type=jnp.float32).astype(jnp.bfloat16)


def solution(mesh):
    act_spec = P(("dp", "ty"), None, "tx")
    col_spec = P("tx", "ty")
    row_spec = P("ty", "tx")

    def layer_fn(x_blk, w_q, w_k, w_v, w_o, w_gate, w_up, w_down):
        wq, wk, wv, wg, wu = (lax.all_gather(w, "tx", axis=0, tiled=True) for w in (w_q, w_k, w_v, w_gate, w_up))
        wo, wd = (lax.all_gather(w, "tx", axis=1, tiled=True) for w in (w_o, w_down))
        x_tok = lax.all_to_all(x_blk, "tx", split_axis=1, concat_axis=2, tiled=True)
        normed_all = lax.all_gather(norm_full(x_tok), "ty", axis=0, tiled=True)
        qkv = jnp.concatenate([project(normed_all, w) for w in (wq, wk, wv)], axis=-1)
        qkv = lax.all_to_all(qkv, "tx", split_axis=0, concat_axis=1, tiled=True)
        n_seqs, seq_len, three = qkv.shape
        q_h, k_h, v_h = (t.reshape(n_seqs, seq_len, -1, HEAD_DIM) for t in jnp.split(qkv, 3, axis=-1))
        heads = causal_attention(rotary(q_h), rotary(k_h), v_h).reshape(n_seqs, seq_len, three // 3)
        heads = lax.all_to_all(heads, "tx", split_axis=1, concat_axis=0, tiled=True)
        attn_out = lax.psum_scatter(project(heads, wo), "ty", scatter_dimension=0, tiled=True)
        resid_h = (x_tok.astype(jnp.float32) + attn_out.astype(jnp.float32)).astype(jnp.bfloat16)
        normed_mlp = lax.all_gather(norm_full(resid_h), "ty", axis=0, tiled=True)
        gate, up = project(normed_mlp, wg), project(normed_mlp, wu)
        act = (jax.nn.silu(gate.astype(jnp.float32)) * up.astype(jnp.float32)).astype(jnp.bfloat16)
        mlp_out = lax.psum_scatter(project(act, wd), "ty", scatter_dimension=0, tiled=True)
        y_tok = (resid_h.astype(jnp.float32) + mlp_out.astype(jnp.float32)).astype(jnp.bfloat16)
        return lax.all_to_all(y_tok, "tx", split_axis=2, concat_axis=1, tiled=True)

    return jax.shard_map(layer_fn, mesh=mesh, in_specs=(act_spec, col_spec, col_spec, col_spec, row_spec, col_spec, col_spec, row_spec), out_specs=act_spec, check_vma=False)
```

time: 935 us -> 678 us (0.73)
  waiting for transfers between devices: 688 us -> 473 us
  matrix products: 102 us -> 61.9 us
  other arithmetic: 72.9 us -> 44.4 us
  blocking collectives: 27.4 us -> 47.5 us
    psum x2 -> x0, waiting for transfers between devices: 379 us -> none  [the longest x1 237 us: layer_fn(): lax.psum((project(normed_mlp, w_gate), project(normed_mlp, w_up)), 'tx')]
    all_gather x2 -> x9, waiting for transfers between devices: 141 us -> 281 us  [the longest x5 107 us: layer_fn(): lax.all_gather(w, 'tx', axis=0, tiled=True)]
    all_to_all x0 -> x3, blocking collectives: none -> 47.5 us  [the longest x1 17.8 us: layer_fn(): x_tok = lax.all_to_all(x_blk, 'tx', split_axis=1, concat_axis=2, tiled=True)]
    dot_general x8 -> x2, matrix products: 34.1 us -> 1.27 us  [the longest x1 0.8 us: causal_attention(): jnp.einsum('nqhd,nkhd->nhqk', q_heads, k_heads, preferred_element_type=jn...]
    psum x2 -> x0, blocking collectives: 27.4 us -> none  [norm_sharded(): moments = lax.psum(moments, 'tx')]
    unnamed x0 -> x2, other arithmetic: none -> 26.3 us
    sub x4 -> x1, other arithmetic: 23.8 us -> 2.11 us  [causal_attention(): prob = jax.nn.softmax(scores, axis=-1).astype(jnp.bfloat16)]
    all_to_all x0 -> x1, waiting for transfers between devices: none -> 20.1 us  [layer_fn(): qkv = lax.all_to_all(qkv, 'tx', split_axis=0, concat_axis=1, tiled=True)]
  transfers between devices with their start and end apart: 6 -> 12, of which waited for: 6 -> 10; matrix products, arithmetic and copies ran while one was open for 0% -> 11% of each run, Pallas kernels for 0% -> 0%
where the time goes in v1:
time: 678 us; the launch traced here: 670 us
  waiting for transfers between devices  473 us (70%)
  matrix products  61.9 us (9%)
  blocking collectives  47.5 us (7%)
  other arithmetic  44.4 us (7%)
  local copies, waits for them, and re-layouts  24.8 us (4%)
  between operations  13.9 us (2%)
    unnamed x13, waiting for transfers between devices  172 us
    all_gather x5, waiting for transfers between devices, layer_fn(): lax.all_gather(w, 'tx', axis=0, tiled=True)  107 us
    all_gather x1, waiting for transfers between devices, layer_fn(): normed_all = lax.all_gather(norm_full(x_tok), 'ty', axis=0, tiled=True)  73.8 us
    all_gather x1, waiting for transfers between devices, layer_fn(): normed_mlp = lax.all_gather(norm_full(resid_h), 'ty', axis=0, tiled=True)  72.4 us
    dot_general x7, matrix products, project(): jnp.einsum('...c,ch->...h', rows_bf, weight, preferred_element_type=jnp.f...  60.6 us
    all_gather x2, waiting for transfers between devices, layer_fn(): lax.all_gather(w, 'tx', axis=1, tiled=True)  28.1 us
    unnamed x2, other arithmetic  26.3 us
    all_to_all x1, waiting for transfers between devices, layer_fn(): qkv = lax.all_to_all(qkv, 'tx', split_axis=0, concat_axis=1, tiled=True)  20.1 us
  transfers between devices with their start and end apart: 12, of which 10 were waited for; matrix products, arithmetic and copies ran while one was open for 11% of the time, Pallas kernels for 0%

profile of v1, /device:TPU:1, one launch (start us, length us, event | category | flops | bytes accessed | tf_op | source)
XLA Modules:
  0.0 669.6 jit_solution(5647380767020361363)
XLA Ops:
  6.5 0.7 all-gather.12.cloned.1.call-update
  7.3 1.9 copy.99
  9.2 0.5 broadcast.143
  9.7 3.7 reduce.13
  13.4 0.4 reshape.209
  13.8 17.8 %all_to_all.63 = bf16[8,2,16384]{2,1,0:T(2,128)(2,1)S(1)} all-to-all(bf16[8,2,16384]{2,1,0:T(2,128)(2,1)S(1)} %reshape.209), channel_id=1, replica_groups=mesh['dp'=1,'ty'=16,'tx'=8] {'tx'}, dimensions={0} | all-to-all | bytes 1048576 | tf_op jit(solution)/shard_map/all_to_all | solution.py:52
  31.6 0.5 reshape.210
  32.1 3.1 convert_reduce_fusion.1
  35.4 1.1 bitcast_convert_fusion
  36.5 0.6 copy.76
  37.3 1.0 multiply_convert_fusion
  38.3 0.7 all-gather.14.cloned.1.call-update
  39.0 0.2 all-gather.16.cloned.1.call-start
  39.3 0.3 all-gather.16.cloned.1.call-update
  39.6 73.8 %all-gather.10.cloned.1.call-done = bf16[16,64,4096]{2,1,0:T(8,128)(2,1)} async-done(((bf16[1,64,4096]{2,1,0:T(8,128)(2,1)}), bf16[16,64,4096]{2,1,0:T(8,128)(2,1)}) %all-gather.10.cloned.1.call-update) | async-done | bytes 8388624 | tf_op jit(solution)/shard_map/all_gather | solution.py:53
  113.4 6.3 fusion.31
  119.7 20.7 %all-gather.14.cloned.1.call-done = bf16[4096,256]{1,0:T(8,128)(2,1)} async-done(((bf16[512,256]{1,0:T(8,128)(2,1)}), bf16[4096,256]{1,0:T(8,128)(2,1)}) %all-gather.14.cloned.1.call-update) | async-done | bytes 2097168 | tf_op jit(solution)/shard_map/all_gather | solution.py:50
  140.4 6.3 fusion.34
  146.7 21.0 %all-gather.16.cloned.1.call-done = bf16[4096,256]{1,0:T(8,128)(2,1)} async-done(((bf16[512,256]{1,0:T(8,128)(2,1)}), bf16[4096,256]{1,0:T(8,128)(2,1)}) %all-gather.16.cloned.1.call-update) | async-done | bytes 2097168 | tf_op jit(solution)/shard_map/all_gather | solution.py:50
  167.7 6.3 fusion.37
  174.0 1.3 pad_maximum_fusion
  175.3 3.8 all-to-all-start.1
  179.0 0.6 all-gather.18.cloned.1.call-update
  179.7 0.8 iota_compare_fusion
  180.5 1.7 fusion.53
  182.1 20.1 %all-to-all-done.1 = bf16[16,64,768]{2,1,0:T(8,128)(2,1)S(1)} async-done(((bf16[16,64,768]{2,1,0:T(8,128)(2,1)}), bf16[16,64,768]{2,1,0:T(8,128)(2,1)S(1)}, u32[]{:S(2)}, u32[]{:S(2)}) %all-to-all-start.1) | async-done | bytes 1572896 | tf_op jit(solution)/shard_map/all_to_all | solution.py:55
  202.3 1.4 slice_convert_fusion
  203.7 0.3 copy.79
  204.2 0.3 copy.93
  204.5 1.3 copy.94
  205.8 1.6 copy.82
  207.4 1.1 fusion.57
  208.5 2.5 copy.95
  210.9 2.4 copy.96
  213.3 2.1 copy.78
  215.4 2.1 subtract_convert_fusion
  217.5 0.8 fusion.45
  218.4 2.1 fusion.59
  220.6 0.5 fusion.40
  221.1 0.5 copy.86
  221.5 14.0 %all_to_all.64 = bf16[2,512,256]{2,0,1:T(2,128)(2,1)S(1)} all-to-all(bf16[2,512,256]{2,0,1:T(2,128)(2,1)S(1)} %copy.86), channel_id=1, replica_groups=mesh['dp'=1,'ty'=16,'tx'=8] {'tx'}, dimensions={1} | all-to-all | bytes 1048576 | tf_op jit(solution)/shard_map/all_to_all | solution.py:59
  235.7 7.2 %convolution_convert_fusion.1 = bf16[16,64,4096]{2,1,0:T(8,128)(2,1)} fusion(bf16[16,64,256]{2,1,0:T(8,128)(2,1)S(1)} %bitcast.89, bf16[256,4096]{1,0:T(8,128)(2,1)} %all-gather.18.cloned.1.call-done), kind=kOutput, calls=%fused_computation.2 | convolution fusion | flops 2151677952 | bytes 11010048 | tf_op jit(solution)/shard_map/...c,ch->...h/dot_general | solution.py:41
  242.9 0.7 all-gather.24.cloned.1.call-update
  243.7 83.7 %reduce-scatter.7.cloned.1.call-done = bf16[1,64,4096]{2,1,0:T(8,128)(2,1)} async-done(((bf16[16,64,4096]{2,1,0:T(8,128)(2,1)}), bf16[1,64,4096]{2,1,0:T(8,128)(2,1)}) %reduce-scatter.7.cloned.1.call-update) | async-done | bytes 524304
  327.4 1.3 convert_reduce_fusion
  328.7 1.0 fusion.42
  329.8 0.7 all-gather.22.cloned.1.call-update
  330.5 0.5 all-gather.26.cloned.1.call-update
  331.1 37.0 %all-gather.24.cloned.1.call-done = bf16[4096,688]{0,1:T(8,128)(2,1)} async-done(((bf16[512,688]{0,1:T(8,128)(2,1)}), bf16[4096,688]{0,1:T(8,128)(2,1)}) %all-gather.24.cloned.1.call-update) | async-done | bytes 5636112 | tf_op jit(solution)/shard_map/all_gather | solution.py:50
  368.1 72.4 %all-gather.20.cloned.1.call-done = bf16[16,64,4096]{2,1,0:T(8,128)(2,1)} async-done(((bf16[1,64,4096]{2,1,0:T(8,128)(2,1)}), bf16[16,64,4096]{2,1,0:T(8,128)(2,1)}) %all-gather.20.cloned.1.call-update) | async-done | bytes 8388624 | tf_op jit(solution)/shard_map/all_gather | solution.py:62
  440.5 11.7 %fusion.28 = bf16[16,64,688]{2,1,0:T(8,128)(2,1)} fusion(bf16[16,64,4096]{2,1,0:T(8,128)(2,1)} %all-gather.20.cloned.1.call-done, bf16[4096,688]{0,1:T(8,128)(2,1)} %all-gather.24.cloned.1.call-done), kind=kOutput, calls=%fused_computation.35 | convolution fusion | flops 5772066816 | bytes 15433728 | tf_op jit(solution)/shard_map/...c,ch->...h/dot_general | solution.py:41
  452.3 28.0 %all-gather.22.cloned.1.call-done = bf16[4096,688]{0,1:T(8,128)(2,1)} async-done(((bf16[512,688]{0,1:T(8,128)(2,1)}), bf16[4096,688]{0,1:T(8,128)(2,1)}) %all-gather.22.cloned.1.call-update) | async-done | bytes 5636112 | tf_op jit(solution)/shard_map/all_gather | solution.py:50
  480.3 11.4 %fusion.11 = bf16[16,64,688]{2,1,0:T(8,128)(2,1)S(1)} fusion(bf16[16,64,688]{2,1,0:T(8,128)(2,1)} %fusion.28, bf16[16,64,4096]{2,1,0:T(8,128)(2,1)} %all-gather.20.cloned.1.call-done, bf16[4096,688]{0,1:T(8,128)(2,1)} %all-gather.22.cloned.1.call-done), kind=kOutput, calls=%fused_computation.18 | convolution fusion | flops 5777702912 | bytes 16842752 | tf_op jit(solution)/shard_map/...c,ch->...h/dot_general | solution.py:41
  491.7 28.1 %all-gather.26.cloned.1.call-done = bf16[688,4096]{1,0:T(8,128)(2,1)} async-done(((bf16[688,512]{1,0:T(8,128)(2,1)}), bf16[688,4096]{1,0:T(8,128)(2,1)}) %all-gather.26.cloned.1.call-update) | async-done | bytes 5636112 | tf_op jit(solution)/shard_map/all_gather | solution.py:51
  519.8 11.5 %convolution_convert_fusion = bf16[16,64,4096]{2,1,0:T(8,128)(2,1)} fusion(bf16[16,64,688]{2,1,0:T(8,128)(2,1)S(1)} %fusion.11, bf16[688,4096]{1,0:T(8,128)(2,1)} %all-gather.26.cloned.1.call-done), kind=kOutput, calls=%fused_computation.1 | convolution fusion | flops 5775556608 | bytes 15433728 | tf_op jit(solution)/shard_map/...c,ch->...h/dot_general | solution.py:41
  531.2 83.8 %reduce-scatter.9.cloned.1.call-done = bf16[1,64,4096]{2,1,0:T(8,128)(2,1)} async-done(((bf16[16,64,4096]{2,1,0:T(8,128)(2,1)}), bf16[1,64,4096]{2,1,0:T(8,128)(2,1)}) %reduce-scatter.9.cloned.1.call-update) | async-done | bytes 524304
  615.0 1.2 fusion.44
  616.2 2.8 copy.89
  619.0 22.6 %reduce.14 = bf16[4096,64]{1,0:T(8,128)(2,1)S(1)} reduce(bf16[4096,1,64]{2,1,0:T(2,128)(2,1)S(1)} %bitcast.79, bf16[]{:T(256)} %broadcast.143), dimensions={1}, to_apply=%bitcast.63.reduce_sub_computation | reduce | bytes 1048578
  641.5 0.7 reshape.211
  642.3 15.7 %all_to_all.65 = bf16[8,2,16384]{2,1,0:T(2,128)(2,1)S(1)} all-to-all(bf16[8,2,16384]{2,1,0:T(2,128)(2,1)S(1)} %reshape.211), channel_id=1, replica_groups=mesh['dp'=1,'ty'=16,'tx'=8] {'tx'}, dimensions={0} | all-to-all | bytes 1048576 | tf_op jit(solution)/shard_map/all_to_all | solution.py:67
  657.9 1.2 reshape.212
  659.2 2.3 copy.90
  661.7 0.9 copy.91
  (36 shorter events, 1.5 us)
Async XLA Ops:
  6.5 33.1 %all-gather.12.cloned.1.call-start = ((), (), s32[]{:S(2)}) async-start(), calls=%async_computation.7 | async-start | bytes 2359296 | tf_op jit(solution)/shard_map/all_gather | solution.py:50
  7.3 106.2 %all-gather.10.cloned.1.call-start = ((), (), s32[]{:S(2)}) async-start(), calls=%async_computation.6 | async-start | bytes 8912896 | tf_op jit(solution)/shard_map/all_gather | solution.py:53
  38.3 102.1 %all-gather.14.cloned.1.call-start = ((), (), s32[]{:S(2)}) async-start(), calls=%async_computation.8 | async-start | bytes 2359296 | tf_op jit(solution)/shard_map/all_gather | solution.py:50
  39.0 128.6 %all-gather.16.cloned.1.call-start = ((), (), s32[]{:S(2)}) async-start(), calls=%async_computation.9 | async-start | bytes 2359296 | tf_op jit(solution)/shard_map/all_gather | solution.py:50
  175.3 27.0 %all-to-all-start.1 = ((bf16[16,64,768]{2,1,0:T(8,128)(2,1)}), bf16[16,64,768]{2,1,0:T(8,128)(2,1)S(1)}, u32[]{:S(2)}, u32[]{:S(2)}) async-start(bf16[16,64,768]{2,1,0:T(8,128)(2,1)} %pad_maximum_fusion), calls=%async_computation.1 | async-start | bytes 3145728 | tf_op jit(solution)/shard_map/all_to_all | solution.py:55
  179.0 56.6 %all-gather.18.cloned.1.call-start = ((), (), s32[]{:S(2)}) async-start(), calls=%async_computation.10 | async-start | bytes 2359296 | tf_op jit(solution)/shard_map/all_gather | solution.py:51
  179.6 147.8 %reduce-scatter.7.cloned.1.call-start = ((), (), s32[]{:S(2)}) async-start(), calls=%async_computation.15 | async-start | bytes 8912896
  208.5 6.9 %copy-start = (f32[2,512,2,64]{3,1,2,0:T(8,128)S(1)}, f32[2,512,2,64]{3,1,2,0:T(8,128)}, u32[]{:S(2)}) copy-start(f32[2,512,2,64]{3,1,2,0:T(8,128)} %copy.94) | copy-start | bytes 1572868
  217.5 1.0 copy-start.2
  218.4 2.1 copy-start.1
  242.9 125.3 %all-gather.24.cloned.1.call-start = ((), (), s32[]{:S(2)}) async-start(), calls=%async_computation.13 | async-start | bytes 6340608 | tf_op jit(solution)/shard_map/all_gather | solution.py:50
  243.6 196.9 %all-gather.20.cloned.1.call-start = ((), (), s32[]{:S(2)}) async-start(), calls=%async_computation.11 | async-start | bytes 8912896 | tf_op jit(solution)/shard_map/all_gather | solution.py:62
  329.7 150.5 %all-gather.22.cloned.1.call-start = ((), (), s32[]{:S(2)}) async-start(), calls=%async_computation.12 | async-start | bytes 6340608 | tf_op jit(solution)/shard_map/all_gather | solution.py:50
  330.5 189.3 %all-gather.26.cloned.1.call-start = ((), (), s32[]{:S(2)}) async-start(), calls=%async_computation.14 | async-start | bytes 6340608 | tf_op jit(solution)/shard_map/all_gather | solution.py:51
  331.1 283.9 %reduce-scatter.9.cloned.1.call-start = ((), (), s32[]{:S(2)}) async-start(), calls=%async_computation.16 | async-start | bytes 8912896
Sparse Core Ops, SparseCore 0:
  9.0 30.2 all-gather.11
  41.5 71.8 all-gather.9
  115.1 25.2 all-gather.13
  142.0 25.6 all-gather.15
  181.2 29.2 all-gather.17
  243.0 84.3 reduce-scatter.6
  329.1 39.0 all-gather.23
  370.3 70.2 all-gather.19
  442.2 37.9 all-gather.21
  481.8 37.9 all-gather.25
  531.4 83.6 reduce-scatter.8

commit v2 on v1

v2 whole, which is shorter than its diff:
```python
import functools

import numpy as np
import jax
import jax.numpy as jnp
from jax import lax
from jax.experimental import pallas as pl
from jax.experimental.pallas import tpu as pltpu
from jax.sharding import PartitionSpec as P

HEAD_DIM = 128
EPS = 1e-5
THETA = 10000.0
RING = 4
MESH = pl.DeviceIdType.MESH
BF16 = jnp.bfloat16
F32 = jnp.float32
AWAY = (0, -1, 1, 2)
NEAR_LAST = (2, -1, 1, 0)


def wrap(v, n):
    return lax.rem(v + 2 * n, n)


class Torus:
    def __init__(self):
        t = lax.axis_index("ty")
        self.me = t
        self.pos = (lax.div(t, RING), lax.rem(t, RING))

    def slot(self, first, a_off, b_off):
        a = wrap(self.pos[first] + a_off, RING)
        b = wrap(self.pos[1 - first] + b_off, RING)
        return a * RING + b if first == 0 else b * RING + a


def entry_barrier(tor, tx_count):
    sem = pltpu.get_barrier_semaphore()
    for first in (0, 1):
        for d in (1, -1):
            pl.semaphore_signal(sem, inc=1, device_id={"ty": tor.slot(first, d, 0)}, device_id_type=MESH)
    me = lax.axis_index("tx")
    for k in range(1, tx_count):
        pl.semaphore_signal(sem, inc=1, device_id={"tx": lax.rem(me + k, tx_count)}, device_id_type=MESH)
    pl.semaphore_wait(sem, 4 + tx_count - 1)


def remote(src, dst, ssem, rsem, device):
    return pltpu.make_async_remote_copy(src_ref=src, dst_ref=dst, send_sem=ssem, recv_sem=rsem, device_id=device, device_id_type=MESH)


class Gather:
    SEMS = 40

    def __init__(self, tor, buf, ssem, rsem):
        self.tor, self.buf, self.ssem, self.rsem = tor, buf, ssem, rsem
        self.q = buf.shape[1] // 4

    def first(self, c):
        return 1 if c == 0 else 0

    def rows(self, c, d, half):
        if not half:
            return pl.ds(c * 2 * self.q, 2 * self.q)
        return pl.ds(c * 2 * self.q + (0 if d == 1 else self.q), self.q)

    def sem(self, c, ph, off, d, half):
        base = c * 20 + (0 if ph == 1 else 4 + 4 * AWAY.index(off))
        return base + (0 if d == 1 else 2) + (1 if half else 0)

    def copy(self, c, ph, off, d, half, hops):
        first = self.first(c)
        back = -d * hops
        s = self.tor.slot(first, back, 0) if ph == 1 else self.tor.slot(first, off, back)
        to = self.tor.slot(first, d, 0) if ph == 1 else self.tor.slot(first, 0, d)
        view = self.buf.at[s, self.rows(c, d, half)]
        i = self.sem(c, ph, off, d, half)
        return remote(view, view, self.ssem.at[i], self.rsem.at[i], {"ty": to})

    def send(self, c, ph, off, d, half=False):
        self.copy(c, ph, off, d, half, 1 if half else 0).start()

    def recv(self, c, ph, off, d, half=False):
        self.copy(c, ph, off, d, half, 2 if half else 1).wait_recv()

    def start(self):
        for ph in (1, 2):
            for c in (0, 1):
                for d in (1, -1):
                    self.send(c, ph, 0, d)

    def near(self):
        for d in (1, -1):
            for c in (0, 1):
                self.recv(c, 1, 0, d)
                self.send(c, 1, 0, d, True)
                self.send(c, 2, -d, 1)
                self.send(c, 2, -d, -1)

    def relay(self, off):
        for d in (1, -1):
            for c in (0, 1):
                self.recv(c, 2, off, d)
                self.send(c, 2, off, d, True)

    def far(self):
        for c in (0, 1):
            for d in (1, -1):
                self.recv(c, 1, 0, d, True)
            for d in (1, -1):
                self.send(c, 2, 2, d)

    def halves(self, off):
        for c in (0, 1):
            for d in (1, -1):
                self.recv(c, 2, off, d, True)

    def drain(self):
        for c in (0, 1):
            for d in (1, -1):
                for half in (False, True):
                    self.copy(c, 1, 0, d, half, 1 if half else 0).wait_send()
                    for off in AWAY:
                        self.copy(c, 2, off, d, half, 1 if half else 0).wait_send()


def add_rows(dst, srcs, width=512):
    d = dst.shape[-1]
    width = min(width, d)

    @pl.loop(0, d // width)
    def _(i):
        cols = pl.ds(pl.multiple_of(i * width, width), width)
        tot = srcs[0][:, cols].astype(F32)
        for s in srcs[1:]:
            tot += s[:, cols].astype(F32)
        dst[:, cols] = tot.astype(dst.dtype)


class Scatter:
    SEMS = 60

    @staticmethod
    def buffers(tok, d):
        q = tok // 4
        return [
            pltpu.VMEM((2, 4, 2, q, d), BF16),
            pltpu.VMEM((2, 4, 2, 2 * q, d), BF16),
            pltpu.VMEM((2, 3, 2 * q, d), BF16),
            pltpu.VMEM((2, 2, q, d), BF16),
            pltpu.VMEM((2, 2, 2 * q, d), BF16),
            pltpu.SemaphoreType.DMA((Scatter.SEMS,)),
            pltpu.SemaphoreType.DMA((Scatter.SEMS,)),
        ]

    def __init__(self, tor, part, bufs):
        self.tor, self.part = tor, part
        self.h1, self.f1, self.mid, self.h2, self.f2, self.ssem, self.rsem = bufs
        self.q = part.shape[1] // 4

    def copy(self, c, ph, bi, d, kind):
        q, first = self.q, c
        di = 0 if d == 1 else 1
        h = di if kind in (0, 2) else 1 - di
        step = 2 * d if kind == 0 else d
        if ph == 1:
            i = c * 30 + bi * 6 + di * 3 + kind
            src = self.part.at[self.tor.slot(first, step, NEAR_LAST[bi]), pl.ds(c * 2 * q + h * q, q)]
            dst = self.h1.at[c, bi, di] if kind == 0 else self.f1.at[c, bi, di, pl.ds(h * q, q)]
            to = self.tor.slot(first, d, 0)
        else:
            i = c * 30 + 24 + di * 3 + kind
            src = self.mid.at[c, 0 if kind == 0 else NEAR_LAST.index(d), pl.ds(h * q, q)]
            dst = self.h2.at[c, di] if kind == 0 else self.f2.at[c, di, pl.ds(h * q, q)]
            to = self.tor.slot(first, 0, d)
        return remote(src, dst, self.ssem.at[i], self.rsem.at[i], {"ty": to})

    def issue(self, bi):
        for kind in (0, 1):
            for c in (0, 1):
                for d in (1, -1):
                    self.copy(c, 1, bi, d, kind).start()

    def augment(self, bi):
        q = self.q
        for c in (0, 1):
            for d in (1, -1):
                di = 0 if d == 1 else 1
                self.copy(c, 1, bi, d, 0).wait_recv()
                mine = self.part.at[self.tor.slot(c, d, NEAR_LAST[bi]), pl.ds(c * 2 * q + di * q, q)]
                add_rows(mine, [mine, self.h1.at[c, bi, di]])
                self.copy(c, 1, bi, d, 2).start()

    def arrived(self, bi):
        q = self.q
        for c in (0, 1):
            for d in (1, -1):
                for kind in (1, 2):
                    self.copy(c, 1, bi, d, kind).wait_recv()
            if bi == 3:
                continue
            own = self.part.at[self.tor.slot(c, 0, NEAR_LAST[bi]), pl.ds(c * 2 * q, 2 * q)]
            add_rows(self.mid.at[c, bi], [own, self.f1.at[c, bi, 0], self.f1.at[c, bi, 1]])
            if bi == 0:
                for d in (1, -1):
                    self.copy(c, 2, 0, d, 0).start()
            else:
                self.copy(c, 2, 0, NEAR_LAST[bi], 1).start()

    def augment2(self):
        q = self.q
        for c in (0, 1):
            for d in (1, -1):
                di = 0 if d == 1 else 1
                self.copy(c, 2, 0, d, 0).wait_recv()
                mine = self.mid.at[c, NEAR_LAST.index(d), pl.ds(di * q, q)]
                add_rows(mine, [mine, self.h2.at[c, di]])
                self.copy(c, 2, 0, d, 2).start()

    def run(self):
        self.issue(0)
        self.issue(1)
        self.augment(0)
        self.issue(2)
        self.augment(1)
        self.issue(3)
        self.arrived(0)
        self.augment(2)
        self.arrived(1)
        self.augment(3)
        self.arrived(2)
        self.augment2()
        self.arrived(3)
        for c in (0, 1):
            for d in (1, -1):
                for kind in (1, 2):
                    self.copy(c, 2, 0, d, kind).wait_recv()

    def finish(self, resid, out):
        q, d = self.q, out.shape[-1]
        width = min(512, d)
        for c in (0, 1):
            rows = pl.ds(c * 2 * q, 2 * q)

            @pl.loop(0, d // width)
            def _(i):
                cols = pl.ds(pl.multiple_of(i * width, width), width)
                tot = self.part[self.tor.me, rows, cols].astype(F32)
                for di in (0, 1):
                    tot += self.f1[c, 3, di, :, cols].astype(F32)
                for di in (0, 1):
                    tot += self.f2[c, di, :, cols].astype(F32)
                tot = tot.astype(BF16).astype(F32)
                out[rows, cols] = (resid[rows, cols].astype(F32) + tot).astype(BF16)

    def drain(self):
        for c in (0, 1):
            for d in (1, -1):
                for kind in (0, 1, 2):
                    self.copy(c, 2, 0, d, kind).wait_send()
                    for bi in range(4):
                        self.copy(c, 1, bi, d, kind).wait_send()


class Exchange:
    def __init__(self, tx_count, src, dst, ssem, rsem):
        self.n, self.src, self.dst, self.ssem, self.rsem = tx_count, src, dst, ssem, rsem
        self.me = lax.axis_index("tx")

    def copy(self, k, sending):
        p = lax.rem(self.me + k, self.n) if sending else self.me
        owner = self.me if sending else lax.rem(self.me + self.n - k, self.n)
        return remote(self.src(p), self.dst(owner), self.ssem.at[k], self.rsem.at[k], {"tx": p})

    def start(self):
        for k in range(1, self.n):
            self.copy(k, True).start()
        self.local().start()

    def local(self):
        return pltpu.make_async_copy(self.src(self.me), self.dst(self.me), self.rsem.at[0])

    def wait(self):
        self.local().wait()
        for k in range(1, self.n):
            self.copy(k, False).wait_recv()

    def drain(self):
        for k in range(1, self.n):
            self.copy(k, True).wait_send()


def norm_rows(src, dst):
    tok, d = src.shape
    step = 16

    @pl.loop(0, tok // step)
    def _(i):
        rows = pl.ds(pl.multiple_of(i * step, step), step)
        v = src[rows, :].astype(F32)
        mean = jnp.sum(v, axis=-1, keepdims=True) * (1.0 / d)
        var = jnp.sum(v * v, axis=-1, keepdims=True) * (1.0 / d) - mean * mean
        dst[rows, :] = ((v - mean) * lax.rsqrt(var + EPS)).astype(BF16)


def gather_kernel(tx_count, x_ref, tok_ref, all_ref, xt, buf, xs, xr, gs, gr, out_sem):
    tok, d = xt.shape
    dx = x_ref.shape[1]
    tor = Torus()
    entry_barrier(tor, tx_count)
    ex = Exchange(
        tx_count,
        lambda p: x_ref.at[pl.ds(pl.multiple_of(p * tok, tok), tok)],
        lambda o: xt.at[:, pl.ds(pl.multiple_of(o * dx, dx), dx)],
        xs,
        xr,
    )
    ex.start()
    ex.wait()
    norm_rows(xt, buf.at[tor.me])
    g = Gather(tor, buf, gs, gr)
    g.start()
    tok_ref[...] = xt[...]
    g.near()
    g.relay(0)
    g.far()
    g.relay(-1)
    g.relay(1)
    g.halves(0)
    g.relay(2)
    g.halves(-1)
    g.halves(1)
    g.halves(2)
    out = pltpu.make_async_copy(buf, all_ref, out_sem)
    out.start()
    ex.drain()
    g.drain()
    out.wait()


def attention_kernel(tx_count, hc, all_ref, w_ref, tok_ref, cos_ref, sin_ref, h_ref, xp, w, acc, qs, qr, kv, hs, hr, load_sem, es, er, os_, or_, *rs_bufs):
    n_dev, tok, d = xp.shape
    dx = w.shape[1]
    seq = tok * tx_count
    spd = n_dev // tx_count
    heads = hc // HEAD_DIM
    tor = Torus()
    w_load = pltpu.make_async_copy(w_ref, w, load_sem.at[4])
    w_load.start()
    x_loads = [pltpu.make_async_copy(all_ref.at[pl.ds(4 * m, 4)], xp.at[pl.ds(4 * m, 4)], load_sem.at[m]) for m in range(4)]
    for cp in x_loads:
        cp.start()
    entry_barrier(tor, tx_count)
    w_load.wait()
    for cp in x_loads:
        cp.wait()
    rows = 4 * tok

    @pl.loop(0, n_dev // 4)
    def _(m):
        slots = pl.ds(m * 4, 4)

        @pl.loop(0, tx_count)
        def _(x):
            lhs = xp[slots, :, pl.ds(pl.multiple_of(x * dx, dx), dx)].reshape(rows, dx)
            part = jnp.dot(lhs, w[x, :, pl.ds(0, 3 * hc)], preferred_element_type=F32)

            @pl.when(x == 0)
            def _():
                acc[...] = part

            @pl.when(x > 0)
            def _():
                acc[...] += part

        qs[slots] = acc[...].astype(BF16).reshape(4, tok, 3 * hc)

    ex = Exchange(
        tx_count,
        lambda p: qs.at[pl.ds(p * spd, spd)],
        lambda o: qr.at[o],
        es,
        er,
    )
    ex.start()
    ex.wait()
    block = min(seq, 128)

    @pl.loop(0, spd)
    def _(s):
        for hd in range(heads):
            def part(which):
                return qr[:, s, :, pl.ds(which * hc + hd * HEAD_DIM, HEAD_DIM)].reshape(seq, HEAD_DIM)

            for which in (0, 1):
                v = part(which).astype(F32)
                rot = v * cos_ref[...] + pltpu.roll(v, HEAD_DIM // 2, 1) * sin_ref[...]
                kv[which] = rot.astype(BF16)
            kv[2] = part(2)
            for b in range(seq // block):
                keys = (b + 1) * block
                sc = lax.dot_general(kv[0, pl.ds(b * block, block)], kv[1, pl.ds(0, keys)], (((1,), (1,)), ((), ())), preferred_element_type=F32)
                sc = sc * HEAD_DIM ** -0.5
                q_pos = b * block + lax.broadcasted_iota(jnp.int32, (block, keys), 0)
                k_pos = lax.broadcasted_iota(jnp.int32, (block, keys), 1)
                sc = jnp.where(q_pos >= k_pos, sc, -1e30)
                e = jnp.exp(sc - jnp.max(sc, axis=-1, keepdims=True))
                prob = (e / jnp.sum(e, axis=-1, keepdims=True)).astype(BF16)
                o = jnp.dot(prob, kv[2, pl.ds(0, keys)], preferred_element_type=F32).astype(BF16)
                n_p = block // tok
                hs[pl.ds(b * n_p, n_p), s, :, pl.ds(hd * HEAD_DIM, HEAD_DIM)] = o.reshape(n_p, tok, HEAD_DIM)

    oe = Exchange(
        tx_count,
        lambda p: hs.at[p],
        lambda o: hr.at[pl.ds(o * spd, spd)],
        os_,
        or_,
    )
    oe.start()
    oe.wait()

    @pl.loop(0, n_dev // 4)
    def _(m):
        slots = pl.ds(m * 4, 4)
        lhs = hr[slots].reshape(rows, hc)

        @pl.loop(0, tx_count)
        def _(x):
            for j in range(dx // hc):
                o = jnp.dot(lhs, w[x, pl.ds(j * hc, hc), pl.ds(3 * hc, hc)], preferred_element_type=F32)
                cols = pl.ds(pl.multiple_of(x * dx + j * hc, hc), hc)
                xp[slots, :, cols] = o.astype(BF16).reshape(4, tok, hc)

    sc = Scatter(tor, xp, rs_bufs)
    sc.run()
    sc.finish(tok_ref, h_ref)
    sc.drain()
    ex.drain()
    oe.drain()


def mlp_kernel(tx_count, h_ref, w_ref, y_ref, buf, wg, wu, wd, part, act, acc_g, acc_u, yt, yr, load_sem, gs, gr, ys, yrs, *rs_bufs):
    n_dev, tok, d = buf.shape
    fp, dx = wg.shape[1:]
    f = w_ref.shape[2]
    tor = Torus()
    loads = [pltpu.make_async_copy(w_ref.at[:, i], dst.at[:, pl.ds(0, f)], load_sem.at[i]) for i, dst in enumerate((wg, wu, wd))]
    for cp in loads:
        cp.start()
    norm_rows(h_ref, buf.at[tor.me])
    entry_barrier(tor, tx_count)
    g = Gather(tor, buf, gs, gr)
    g.start()
    if fp > f:
        for dst in (wg, wu, wd):
            dst[:, pl.ds(f, fp - f), :] = jnp.zeros((tx_count, fp - f, dx), BF16)
    g.near()
    g.relay(0)
    g.far()
    g.relay(-1)
    g.relay(1)
    g.halves(0)
    g.relay(2)
    g.halves(-1)
    g.halves(1)
    g.halves(2)
    for cp in loads:
        cp.wait()
    rows = 4 * tok

    @pl.loop(0, n_dev // 4)
    def _(m):
        slots = pl.ds(m * 4, 4)

        @pl.loop(0, tx_count)
        def _(x):
            lhs = buf[slots, :, pl.ds(pl.multiple_of(x * dx, dx), dx)].reshape(rows, dx)
            for acc, wt in ((acc_g, wg), (acc_u, wu)):
                val = lax.dot_general(lhs, wt[x], (((1,), (1,)), ((), ())), preferred_element_type=F32)

                @pl.when(x == 0)
                def _():
                    acc[...] = val

                @pl.when(x > 0)
                def _():
                    acc[...] += val

        gate = acc_g[...].astype(BF16).astype(F32)
        up = acc_u[...].astype(BF16).astype(F32)
        act[...] = (gate * jax.nn.sigmoid(gate) * up).astype(BF16)

        @pl.loop(0, tx_count)
        def _(x):
            o = jnp.dot(act[...], wd[x], preferred_element_type=F32)
            part[slots, :, pl.ds(pl.multiple_of(x * dx, dx), dx)] = o.astype(BF16).reshape(4, tok, dx)

    sc = Scatter(tor, part, rs_bufs)
    sc.run()
    sc.finish(h_ref, yt)
    ye = Exchange(
        tx_count,
        lambda p: yt.at[:, pl.ds(pl.multiple_of(p * dx, dx), dx)],
        lambda o: yr.at[pl.ds(pl.multiple_of(o * tok, tok), tok)],
        ys,
        yrs,
    )
    ye.start()
    g.drain()
    sc.drain()
    ye.wait()
    y_ref[...] = yr[...]
    ye.drain()


VMEM_SPEC = pl.BlockSpec(memory_space=pltpu.VMEM)
ANY_SPEC = pl.BlockSpec(memory_space=pl.ANY)


def rotary_tables(seq_len):
    half = HEAD_DIM // 2
    inv_freq = THETA ** (-2.0 * jnp.arange(half, dtype=F32) / HEAD_DIM)
    angles = jnp.arange(seq_len, dtype=F32)[:, None] * inv_freq[None, :]
    cos_t, sin_t = jnp.cos(angles), jnp.sin(angles)
    return jnp.concatenate([cos_t, cos_t], -1), jnp.concatenate([-sin_t, sin_t], -1)


def call(kernel, name, ident, out_shape, in_specs, out_specs, scratch, flops, nbytes):
    return pl.pallas_call(
        kernel,
        name=name,
        out_shape=out_shape,
        in_specs=in_specs,
        out_specs=out_specs,
        scratch_shapes=scratch,
        cost_estimate=pl.CostEstimate(flops=flops, bytes_accessed=nbytes, transcendentals=0),
        compiler_params=pltpu.CompilerParams(collective_id=ident, has_side_effects=True, vmem_limit_bytes=62 * 2**20),
    )


def solution(mesh):
    tx_count, n_dev = mesh.shape["tx"], mesh.shape["ty"]
    act_spec = P(("dp", "ty"), None, "tx")
    col_spec = P("tx", "ty")
    row_spec = P("ty", "tx")
    dma = pltpu.SemaphoreType.DMA

    def layer_fn(x_blk, w_q, w_k, w_v, w_o, w_gate, w_up, w_down):
        seq, dx = x_blk.shape[1:]
        hc, f = w_q.shape[1], w_gate.shape[1]
        tok, d = seq // tx_count, dx * tx_count
        spd = n_dev // tx_count
        fp = -(-f // 128) * 128
        shape = jax.ShapeDtypeStruct
        w_o_rows = w_o.reshape(hc, dx // hc, hc).transpose(1, 0, 2).reshape(dx, hc)
        attn_w = lax.all_gather(jnp.concatenate([w_q, w_k, w_v, w_o_rows], axis=1), "tx", axis=0, tiled=True).reshape(tx_count, dx, 4 * hc)
        mlp_w = lax.all_gather(jnp.concatenate([w_gate.T, w_up.T, w_down], axis=0), "tx", axis=0, tiled=True).reshape(tx_count, 3, f, dx)
        cos_t, sin_t = rotary_tables(seq)

        x_tok, x_all = call(
            functools.partial(gather_kernel, tx_count), "norm_gather", 1,
            (shape((tok, d), BF16), shape((n_dev, tok, d), BF16)),
            [VMEM_SPEC], (VMEM_SPEC, ANY_SPEC),
            [pltpu.VMEM((tok, d), BF16), pltpu.VMEM((n_dev, tok, d), BF16), dma((tx_count,)), dma((tx_count,)),
             dma((Gather.SEMS,)), dma((Gather.SEMS,)), dma],
            2 * n_dev * tok * d * 3 * hc, n_dev * tok * d * 4,
        )(x_blk[0])
        h = call(
            functools.partial(attention_kernel, tx_count, hc), "attention", 2,
            shape((tok, d), BF16),
            [ANY_SPEC, ANY_SPEC, VMEM_SPEC, VMEM_SPEC, VMEM_SPEC], VMEM_SPEC,
            [pltpu.VMEM((n_dev, tok, d), BF16), pltpu.VMEM((tx_count, dx, 4 * hc), BF16), pltpu.VMEM((4 * tok, 3 * hc), F32),
             pltpu.VMEM((n_dev, tok, 3 * hc), BF16), pltpu.VMEM((tx_count, spd, tok, 3 * hc), BF16), pltpu.VMEM((3, seq, HEAD_DIM), BF16),
             pltpu.VMEM((tx_count, spd, tok, hc), BF16), pltpu.VMEM((n_dev, tok, hc), BF16),
             dma((5,)), dma((tx_count,)), dma((tx_count,)), dma((tx_count,)), dma((tx_count,))] + Scatter.buffers(tok, d),
            2 * n_dev * tok * d * 4 * hc, n_dev * tok * d * 4,
        )(x_all, attn_w, x_tok, cos_t, sin_t)
        y = call(
            functools.partial(mlp_kernel, tx_count), "mlp", 3,
            shape((seq, dx), BF16),
            [VMEM_SPEC, ANY_SPEC], VMEM_SPEC,
            [pltpu.VMEM((n_dev, tok, d), BF16)] + [pltpu.VMEM((tx_count, fp, dx), BF16)] * 3
            + [pltpu.VMEM((n_dev, tok, d), BF16), pltpu.VMEM((4 * tok, fp), BF16), pltpu.VMEM((4 * tok, fp), F32), pltpu.VMEM((4 * tok, fp), F32),
               pltpu.VMEM((tok, d), BF16), pltpu.VMEM((seq, dx), BF16), dma((3,)), dma((Gather.SEMS,)), dma((Gather.SEMS,)),
               dma((tx_count,)), dma((tx_count,))] + Scatter.buffers(tok, d),
            2 * n_dev * tok * d * 3 * f, n_dev * tok * d * 4,
        )(h, mlp_w)
        return y[None]

    return jax.shard_map(layer_fn, mesh=mesh, in_specs=(act_spec, col_spec, col_spec, col_spec, row_spec, col_spec, col_spec, row_spec), out_specs=act_spec, check_vma=False)
```

time: 678 us -> 367 us (0.54); the launches traced: 670 us -> 367 us
  waiting for transfers between devices: 473 us -> 0.07 us
  Pallas kernels: 0 us -> 344 us
  matrix products: 61.9 us -> 0 us
  blocking collectives: 47.5 us -> 0 us
  other arithmetic: 44.4 us -> 5.69 us
  local copies, waits for them, and re-layouts: 24.8 us -> 3.07 us
    pallas_call x0 -> x3, Pallas kernels: none -> 344 us  [the longest x1 149 us: layer_fn(): call(functools.partial(mlp_kernel, tx_count), 'mlp', 3, shape((seq, dx),...]
    all_gather x9 -> x2, waiting for transfers between devices: 281 us -> 0.04 us  [the longest x1 0.02 us: layer_fn(): lax.all_gather(jnp.concatenate([w_gate.T, w_up.T, w_down], axis=0), 'tx',...]
    unnamed x13 -> x2, waiting for transfers between devices: 172 us -> 0.03 us
    dot_general x9 -> x0, matrix products: 61.9 us -> none  [the longest x7 60.6 us: project(): jnp.einsum('...c,ch->...h', rows_bf, weight, preferred_element_type=jnp.f...]
    all_to_all x3 -> x0, blocking collectives: 47.5 us -> none  [the longest x1 17.8 us: layer_fn(): x_tok = lax.all_to_all(x_blk, 'tx', split_axis=1, concat_axis=2, tiled=True)]
    unnamed x2 -> x0, other arithmetic: 26.3 us -> none
    all_to_all x1 -> x0, waiting for transfers between devices: 20.1 us -> none  [layer_fn(): qkv = lax.all_to_all(qkv, 'tx', split_axis=0, concat_axis=1, tiled=True)]
    unnamed x17 -> x7, local copies, waits for them, and re-layouts: 12 us -> 1.88 us
  transfers between devices with their start and end apart: 12 -> 2, of which waited for: 10 -> 0; matrix products, arithmetic and copies ran while one was open for 11% -> 1% of each run, Pallas kernels for 0% -> 53%
where the time goes in v2:
time: 367 us
  Pallas kernels  344 us (94%)
  between operations  13.5 us (4%)
  other arithmetic  5.69 us (2%)
    pallas_call x1, Pallas kernels, layer_fn(): call(functools.partial(mlp_kernel, tx_count), 'mlp', 3, shape((seq, dx),...  149 us
    pallas_call x1, Pallas kernels, layer_fn(): call(functools.partial(attention_kernel, tx_count, hc), 'attention', 2, s...  128 us
    pallas_call x1, Pallas kernels, layer_fn(): call(functools.partial(gather_kernel, tx_count), 'norm_gather', 1, (shape...  67 us
  transfers between devices with their start and end apart: 2, of which 0 were waited for; matrix products, arithmetic and copies ran while one was open for 1% of the time, Pallas kernels for 53%

profile of v2, /device:TPU:1, one launch (start us, length us, event | category | flops | bytes accessed | tf_op | source)
XLA Modules:
  0.0 366.6 jit_solution(4888860015225448727)
XLA Ops:
  6.5 0.0 copy-start.2
  6.5 0.0 copy-start.1
  6.5 0.0 copy-start
  6.5 0.0 all-gather.3.cloned.1.call-start
  6.5 1.2 reshape.17
  7.7 2.2 pad_maximum_fusion.1
  10.0 0.0 all-gather.3.cloned.1.call-update
  10.0 0.0 all-gather.5.cloned.1.call-start
  10.1 0.0 copy-done.2
  10.1 0.0 copy-done.1
  10.1 0.0 copy-done
  10.1 1.5 pad_maximum_fusion
  11.5 0.0 all-gather.5.cloned.1.call-update
  11.6 1.0 fusion.2
  12.6 1.0 pad_maximum_fusion.2
  13.6 67.0 %norm_gather.1 = (bf16[64,4096]{1,0:T(8,128)(2,1)}, bf16[16,64,4096]{2,1,0:T(8,128)(2,1)}) custom-call(bf16[512,512]{1,0:T(8,128)(2,1)} %bitcast.15), custom_call_target="tpu_custom_call" | custom-call | flops 6442450944 | bytes 16777216 | tf_op jit(solution)/shard_map/norm_gather/pallas_call | solution.py:562
  80.6 0.0 all-gather.3.cloned.1.call-done
  80.6 128.2 %attention.1.h_ref = bf16[64,4096]{1,0:T(8,128)(2,1)} custom-call(bf16[16,64,4096]{2,1,0:T(8,128)(2,1)} %get-tuple-element.7.all_ref, bf16[8,512,1024]{2,1,0:T(8,128)(2,1)} %bitcast.14, bf16[64,4096]{1,0:T(8,128)(2,1)} %get-tuple-element.8.tok_ref, f32[512,128]{1,0:T(8,128)} %get-tuple-element.12.cos_ref, f32[512,128]{1,0:T(8,128)} %get-tuple-element.13.sin_ref), custom_call_target="tpu_custom_call" | custom-call | flops 8589934592 | bytes 16777216 | tf_op jit(solution)/shard_map/attention/pallas_call | solution.py:570
  208.9 0.0 all-gather.5.cloned.1.call-done
  208.9 149.0 %mlp.1 = bf16[512,512]{1,0:T(8,128)(2,1)} custom-call(bf16[64,4096]{1,0:T(8,128)(2,1)} %attention.1.h_ref, bf16[8,3,688,512]{3,2,1,0:T(8,128)(2,1)} %bitcast.13), custom_call_target="tpu_custom_call" | custom-call | flops 17314086912 | bytes 16777216 | tf_op jit(solution)/shard_map/mlp/pallas_call | solution.py:580
  357.9 1.9 copy.11
  (2 shorter events, 0.0 us)
Async XLA Ops:
  6.5 3.5 copy-start.2
  6.5 3.5 copy-start.1
  6.5 3.5 copy-start
  6.5 74.1 %all-gather.3.cloned.1.call-start = ((), (), s32[]{:S(2)}) async-start(), calls=%async_computation | async-start | bytes 9437184 | tf_op jit(solution)/shard_map/all_gather | solution.py:558
  10.0 198.9 %all-gather.5.cloned.1.call-start = ((), (), s32[]{:S(2)}) async-start(), calls=%async_computation.1 | async-start | bytes 19021824 | tf_op jit(solution)/shard_map/all_gather | solution.py:559
Sparse Core Ops, SparseCore 0:
  10.1 54.1 all-gather.2
  66.0 107.5 all-gather.4

commit v3 on v2

v3 whole, which is shorter than its diff:
```python
import functools

import numpy as np
import jax
import jax.numpy as jnp
from jax import lax
from jax.experimental import pallas as pl
from jax.experimental.pallas import tpu as pltpu
from jax.sharding import PartitionSpec as P

HEAD_DIM = 128
EPS = 1e-5
THETA = 10000.0
RING = 4
MESH = pl.DeviceIdType.MESH
BF16 = jnp.bfloat16
F32 = jnp.float32
AWAY = (0, -1, 1, 2)
ORDER = (-1, 2, 1, 0)


def wrap(v, n):
    return lax.rem(v + 2 * n, n)


class Torus:
    def __init__(self):
        t = lax.axis_index("ty")
        self.me = t
        self.pos = (lax.div(t, RING), lax.rem(t, RING))

    def slot(self, first, a_off, b_off):
        a = wrap(self.pos[first] + a_off, RING)
        b = wrap(self.pos[1 - first] + b_off, RING)
        return a * RING + b if first == 0 else b * RING + a


def entry_barrier(tor, tx_count):
    sem = pltpu.get_barrier_semaphore()
    for first in (0, 1):
        for d in (1, -1):
            pl.semaphore_signal(sem, inc=1, device_id={"ty": tor.slot(first, d, 0)}, device_id_type=MESH)
    me = lax.axis_index("tx")
    for k in range(1, tx_count):
        pl.semaphore_signal(sem, inc=1, device_id={"tx": lax.rem(me + k, tx_count)}, device_id_type=MESH)
    pl.semaphore_wait(sem, 4 + tx_count - 1)


def remote(src, dst, ssem, rsem, device):
    return pltpu.make_async_remote_copy(src_ref=src, dst_ref=dst, send_sem=ssem, recv_sem=rsem, device_id=device, device_id_type=MESH)


class Gather:
    SEMS = 40

    def __init__(self, tor, buf, ssem, rsem):
        self.tor, self.buf, self.ssem, self.rsem = tor, buf, ssem, rsem
        self.q = buf.shape[1] // 4

    def first(self, c):
        return 1 if c == 0 else 0

    def rows(self, c, d, half):
        if not half:
            return pl.ds(c * 2 * self.q, 2 * self.q)
        return pl.ds(c * 2 * self.q + (0 if d == 1 else self.q), self.q)

    def sem(self, c, ph, off, d, half):
        base = c * 20 + (0 if ph == 1 else 4 + 4 * AWAY.index(off))
        return base + (0 if d == 1 else 2) + (1 if half else 0)

    def copy(self, c, ph, off, d, half, hops):
        first = self.first(c)
        back = -d * hops
        s = self.tor.slot(first, back, 0) if ph == 1 else self.tor.slot(first, off, back)
        to = self.tor.slot(first, d, 0) if ph == 1 else self.tor.slot(first, 0, d)
        view = self.buf.at[s, self.rows(c, d, half)]
        i = self.sem(c, ph, off, d, half)
        return remote(view, view, self.ssem.at[i], self.rsem.at[i], {"ty": to})

    def send(self, c, ph, off, d, half=False):
        self.copy(c, ph, off, d, half, 1 if half else 0).start()

    def recv(self, c, ph, off, d, half=False):
        self.copy(c, ph, off, d, half, 2 if half else 1).wait_recv()

    def start(self):
        for ph in (1, 2):
            for c in (0, 1):
                for d in (1, -1):
                    self.send(c, ph, 0, d)

    def near(self):
        for d in (1, -1):
            for c in (0, 1):
                self.recv(c, 1, 0, d)
                self.send(c, 1, 0, d, True)
                self.send(c, 2, -d, 1)
                self.send(c, 2, -d, -1)

    def relay(self, off):
        for d in (1, -1):
            for c in (0, 1):
                self.recv(c, 2, off, d)
                self.send(c, 2, off, d, True)

    def far(self):
        for c in (0, 1):
            for d in (1, -1):
                self.recv(c, 1, 0, d, True)
            for d in (1, -1):
                self.send(c, 2, 2, d)

    def halves(self, off):
        for c in (0, 1):
            for d in (1, -1):
                self.recv(c, 2, off, d, True)

    def drain(self):
        for c in (0, 1):
            for d in (1, -1):
                for half in (False, True):
                    self.copy(c, 1, 0, d, half, 1 if half else 0).wait_send()
                    for off in AWAY:
                        self.copy(c, 2, off, d, half, 1 if half else 0).wait_send()


def add_rows(dst, srcs, width=512):
    d = dst.shape[-1]
    width = min(width, d)

    @pl.loop(0, d // width)
    def _(i):
        cols = pl.ds(pl.multiple_of(i * width, width), width)
        tot = srcs[0][:, cols].astype(F32)
        for s in srcs[1:]:
            tot += s[:, cols].astype(F32)
        dst[:, cols] = tot.astype(dst.dtype)


class Scatter:
    SEMS = 60

    @staticmethod
    def buffers(tok, d):
        q = tok // 4
        return [
            pltpu.VMEM((2, 4, 2, q, d), BF16),
            pltpu.VMEM((2, 4, 2, 2 * q, d), BF16),
            pltpu.VMEM((2, 3, 2 * q, d), BF16),
            pltpu.VMEM((2, 2, q, d), BF16),
            pltpu.VMEM((2, 2, 2 * q, d), BF16),
            pltpu.SemaphoreType.DMA((Scatter.SEMS,)),
            pltpu.SemaphoreType.DMA((Scatter.SEMS,)),
        ]

    def __init__(self, tor, part, bufs):
        self.tor, self.part = tor, part
        self.h1, self.f1, self.mid, self.h2, self.f2, self.ssem, self.rsem = bufs
        self.q = part.shape[1] // 4

    def copy(self, c, ph, bi, d, kind):
        q, first = self.q, c
        di = 0 if d == 1 else 1
        h = di if kind in (0, 2) else 1 - di
        step = 2 * d if kind == 0 else d
        if ph == 1:
            i = c * 30 + bi * 6 + di * 3 + kind
            src = self.part.at[self.tor.slot(first, step, ORDER[bi]), pl.ds(c * 2 * q + h * q, q)]
            dst = self.h1.at[c, bi, di] if kind == 0 else self.f1.at[c, bi, di, pl.ds(h * q, q)]
            to = self.tor.slot(first, d, 0)
        else:
            i = c * 30 + 24 + di * 3 + kind
            src = self.mid.at[c, ORDER.index(2 if kind == 0 else d), pl.ds(h * q, q)]
            dst = self.h2.at[c, di] if kind == 0 else self.f2.at[c, di, pl.ds(h * q, q)]
            to = self.tor.slot(first, 0, d)
        return remote(src, dst, self.ssem.at[i], self.rsem.at[i], {"ty": to})

    def issue(self, bi):
        for kind in (0, 1):
            for c in (0, 1):
                for d in (1, -1):
                    self.copy(c, 1, bi, d, kind).start()

    def augment(self, bi):
        q = self.q
        for c in (0, 1):
            for d in (1, -1):
                di = 0 if d == 1 else 1
                self.copy(c, 1, bi, d, 0).wait_recv()
                mine = self.part.at[self.tor.slot(c, d, ORDER[bi]), pl.ds(c * 2 * q + di * q, q)]
                add_rows(mine, [mine, self.h1.at[c, bi, di]])
                self.copy(c, 1, bi, d, 2).start()

    def arrived(self, bi):
        q = self.q
        for c in (0, 1):
            for d in (1, -1):
                for kind in (1, 2):
                    self.copy(c, 1, bi, d, kind).wait_recv()
            if bi == 3:
                continue
            own = self.part.at[self.tor.slot(c, 0, ORDER[bi]), pl.ds(c * 2 * q, 2 * q)]
            add_rows(self.mid.at[c, bi], [own, self.f1.at[c, bi, 0], self.f1.at[c, bi, 1]])
            if ORDER[bi] == 2:
                for d in (1, -1):
                    self.copy(c, 2, 0, d, 0).start()
            else:
                self.copy(c, 2, 0, ORDER[bi], 1).start()

    def augment2(self):
        q = self.q
        for c in (0, 1):
            for d in (1, -1):
                di = 0 if d == 1 else 1
                self.copy(c, 2, 0, d, 0).wait_recv()
                mine = self.mid.at[c, ORDER.index(d), pl.ds(di * q, q)]
                add_rows(mine, [mine, self.h2.at[c, di]])
                self.copy(c, 2, 0, d, 2).start()

    def run(self, compute, after):
        for bi in (0, 1):
            compute(bi)
            self.issue(bi)
        self.augment(0)
        compute(2)
        self.issue(2)
        self.augment(1)
        compute(3)
        self.issue(3)
        self.arrived(0)
        after(0)
        self.augment(2)
        self.arrived(1)
        after(1)
        self.augment(3)
        self.arrived(2)
        after(2)
        self.augment2()
        self.arrived(3)
        for c in (0, 1):
            for d in (1, -1):
                for kind in (1, 2):
                    self.copy(c, 2, 0, d, kind).wait_recv()
        after(3)

    def finish(self, resid, out):
        q, d = self.q, out.shape[-1]
        width = min(512, d)
        for c in (0, 1):
            rows = pl.ds(c * 2 * q, 2 * q)

            @pl.loop(0, d // width)
            def _(i):
                cols = pl.ds(pl.multiple_of(i * width, width), width)
                tot = self.part[self.tor.me, rows, cols].astype(F32)
                for di in (0, 1):
                    tot += self.f1[c, 3, di, :, cols].astype(F32)
                for di in (0, 1):
                    tot += self.f2[c, di, :, cols].astype(F32)
                tot = tot.astype(BF16).astype(F32)
                out[rows, cols] = (resid[rows, cols].astype(F32) + tot).astype(BF16)

    def drain(self):
        for c in (0, 1):
            for d in (1, -1):
                for kind in (0, 1, 2):
                    self.copy(c, 2, 0, d, kind).wait_send()
                    for bi in range(4):
                        self.copy(c, 1, bi, d, kind).wait_send()


class Exchange:
    def __init__(self, tx_count, src, dst, ssem, rsem):
        self.n, self.src, self.dst, self.ssem, self.rsem = tx_count, src, dst, ssem, rsem
        self.me = lax.axis_index("tx")

    def copy(self, k, sending):
        p = lax.rem(self.me + k, self.n) if sending else self.me
        owner = self.me if sending else lax.rem(self.me + self.n - k, self.n)
        return remote(self.src(p), self.dst(owner), self.ssem.at[k], self.rsem.at[k], {"tx": p})

    def start(self):
        for k in range(1, self.n):
            self.copy(k, True).start()
        self.local().start()

    def local(self):
        return pltpu.make_async_copy(self.src(self.me), self.dst(self.me), self.rsem.at[0])

    def wait(self):
        self.local().wait()
        for k in range(1, self.n):
            self.copy(k, False).wait_recv()

    def drain(self):
        for k in range(1, self.n):
            self.copy(k, True).wait_send()


def norm_rows(src, dst):
    tok, d = src.shape
    step = 16

    @pl.loop(0, tok // step)
    def _(i):
        rows = pl.ds(pl.multiple_of(i * step, step), step)
        v = src[rows, :].astype(F32)
        mean = jnp.sum(v, axis=-1, keepdims=True) * (1.0 / d)
        var = jnp.sum(v * v, axis=-1, keepdims=True) * (1.0 / d) - mean * mean
        dst[rows, :] = ((v - mean) * lax.rsqrt(var + EPS)).astype(BF16)


class Ring:
    SEMS = 9

    def __init__(self, tx_count, rows, src, slot, ssem, rsem, base):
        self.nx, self.rows, self.src, self.slot, self.ssem, self.rsem, self.base = tx_count // 2, rows, src, slot, ssem, rsem, base
        me = lax.axis_index("tx")
        self.me, self.x, self.core = me, lax.div(me, 2), lax.rem(me, 2)
        self.split = (rows // 2 + 15) // 16 * 16

    def tx(self, dx, other=False):
        return wrap(self.x + dx, self.nx) * 2 + (1 - self.core if other else self.core)

    def half(self, view, d):
        return view.at[pl.ds(0, self.split)] if d == 1 else view.at[pl.ds(self.split, self.rows - self.split)]

    def copy(self, i, src, dst, to):
        i += self.base
        return remote(src, dst, self.ssem.at[i], self.rsem.at[i], {"tx": to})

    def pass_on(self, d, recv=False):
        view = self.slot(self.tx(-d if recv else 0))
        return self.copy(0 if d == 1 else 1, view if recv else self.src, view, self.tx(d))

    def relay(self, d, recv=False):
        view = self.half(self.slot(self.tx(-2 * d if recv else -d)), d)
        return self.copy(2 if d == 1 else 3, view, view, self.tx(d))

    def across(self, which, recv=False):
        view = self.slot(self.tx(which, recv))
        if abs(which) == 2:
            view = self.half(view, which // 2)
        src = self.src if which == 0 and not recv else view
        return self.copy(6 + which, src, view, self.tx(0, True))

    def all_across(self):
        return (0, 1, -1, 2, -2) if self.nx > 1 else (0,)

    def own(self):
        return pltpu.make_async_copy(self.src, self.slot(self.me), self.rsem.at[self.base + 8 + 1])

    def start(self, place=True):
        if self.nx > 1:
            for d in (1, -1):
                self.pass_on(d).start()
        self.across(0).start()
        if place:
            self.own().start()

    def step(self):
        if self.nx > 1:
            for d in (1, -1):
                self.pass_on(d, True).wait_recv()
                self.relay(d).start()
                self.across(-d).start()

    def step2(self):
        if self.nx > 1:
            for d in (1, -1):
                self.relay(d, True).wait_recv()
                self.across(2 * d).start()

    def finish(self, place=True):
        for which in self.all_across():
            self.across(which, True).wait_recv()
        if place:
            self.own().wait()

    def drain(self):
        if self.nx > 1:
            for d in (1, -1):
                self.pass_on(d).wait_send()
                self.relay(d).wait_send()
        for which in self.all_across():
            self.across(which).wait_send()


RING_SEMS = 10


def layer_kernel(tx_count, x_ref, wq_ref, wk_ref, wv_ref, wo_ref, wg_ref, wu_ref, wd_ref, cos_ref, sin_ref, y_ref,
                 xp, x2, wqkv, wo, wg, wu, wd, xs, os_, act, kv, xt, h, yr,
                 load_sem, a2a_s, a2a_r, qkv_s, qkv_r, gs, gr, ws, wr, *rs_bufs):
    n_dev, tok, d = xp.shape
    dx = x_ref.shape[1]
    hc = wq_ref.shape[1]
    f, fp = wg_ref.shape[0], wg.shape[2]
    seq = tok * tx_count
    spd = n_dev // tx_count
    heads = hc // HEAD_DIM
    q2 = tok // 2
    c3 = 3 * hc
    tor = Torus()
    me_tx = lax.axis_index("tx")

    def exchange(i, src, dst):
        return Exchange(tx_count, src, dst, a2a_s.at[i], a2a_r.at[i])

    def col(start, width):
        return pl.ds(pl.multiple_of(start, width), width)

    def ring(i, src, slot):
        return Ring(tx_count, src.shape[0], src, slot, ws, wr, i * RING_SEMS)

    rings = [ring(i, src, lambda o, i=i: wqkv.at[o, :, pl.ds(i * hc, hc)]) for i, src in enumerate((wq_ref, wk_ref, wv_ref))]
    rings.append(ring(3, wo_ref, lambda o: wo.at[o]))
    r_gate = ring(4, wg.at[me_tx], lambda o: wg.at[o])
    r_up = ring(5, wu.at[me_tx], lambda o: wu.at[o])
    r_down = ring(6, wd_ref, lambda o: wd.at[o, pl.ds(0, f)])

    raw = [pltpu.make_async_copy(src, wd.at[i, pl.ds(0, f)], load_sem.at[i]) for i, src in enumerate((wg_ref, wu_ref))]
    for cp in raw:
        cp.start()
    entry_barrier(tor, tx_count)
    xe = exchange(
        0,
        lambda p: x_ref.at[pl.ds(pl.multiple_of(p * tok, tok), tok)],
        lambda o: xt.at[:, col(o * dx, dx)],
    )
    xe.start()
    if fp > f:
        wd[:, pl.ds(f, fp - f), :] = jnp.zeros((tx_count, fp - f, dx), BF16)
    xe.wait()
    norm_rows(xt, xp.at[tor.me])
    g1 = Gather(tor, xp, gs, gr)
    g1.start()
    for r in rings:
        r.start()
    for cp in raw:
        cp.wait()
    for i, dst in enumerate((wg, wu)):
        for j in range(fp // 128):
            dst[me_tx, :, pl.ds(j * 128, 128)] = wd[i, pl.ds(j * 128, 128), :].T

    def pieces(off):
        return [(c, tor.slot(1 - c, off, n), (c * 4 + n) * q2) for c in (0, 1) for n in range(RING)]

    def stage(src, off, dst, cols):
        for c, s, at in pieces(off):
            dst[pl.ds(at, q2), :] = src[s, pl.ds(c * q2, q2), cols]

    def qkv_copy(s_owner, k, sl, c, sending, src_slot):
        rows = pl.ds(c * q2, q2)
        i = k * spd * 2 + sl * 2 + c
        src = x2.at[src_slot, rows, pl.ds(0, c3)]
        dst = x2.at[sl * tx_count + s_owner, rows, pl.ds(c3, c3)]
        return src, dst, i

    def qkv_group(off):
        stage(xp, off, xs, pl.ds(0, d))

        @pl.loop(0, 3)
        def _(n):
            cols = col(n * hc, hc)
            out = jnp.dot(xs[...], wqkv[:, :, cols].reshape(d, hc), preferred_element_type=F32).astype(BF16)
            for c, s, at in pieces(off):
                x2[s, pl.ds(c * q2, q2), cols] = out[at : at + q2]

        for c, s, _ in pieces(off):
            p, sl = lax.div(s, spd), lax.rem(s, spd)
            k = lax.rem(p - me_tx + tx_count, tx_count)
            src, dst, i = qkv_copy(me_tx, k, sl, c, True, s)

            @pl.when(k == 0)
            def _():
                pltpu.make_async_copy(src, dst, qkv_r.at[i]).start()

            @pl.when(k != 0)
            def _():
                remote(src, dst, qkv_s.at[i], qkv_r.at[i], {"tx": p}).start()

    g1.near()
    rings[0].step()
    g1.relay(0)
    for r in rings[1:]:
        r.step()
    for r in rings:
        r.step2()
    g1.far()
    g1.relay(-1)
    g1.relay(1)
    g1.halves(0)
    for r in rings[:3]:
        r.finish()
    qkv_group(0)
    g1.relay(2)
    g1.halves(-1)
    qkv_group(-1)
    g1.halves(1)
    qkv_group(1)
    g1.halves(2)
    qkv_group(2)

    for k in range(tx_count):
        owner = lax.rem(me_tx + tx_count - k, tx_count)
        for sl in range(spd):
            for c in (0, 1):
                src, dst, i = qkv_copy(owner, k, sl, c, False, me_tx * spd + sl)
                if k == 0:
                    pltpu.make_async_copy(src, dst, qkv_r.at[i]).wait()
                else:
                    remote(src, dst, qkv_s.at[i], qkv_r.at[i], {"tx": me_tx}).wait_recv()
    block = min(seq, 128)

    @pl.loop(0, spd)
    def _(s):
        for hd in range(heads):
            def part(which):
                return x2[pl.ds(s * tx_count, tx_count), :, pl.ds(c3 + which * hc + hd * HEAD_DIM, HEAD_DIM)].reshape(seq, HEAD_DIM)

            for which in (0, 1):
                v = part(which).astype(F32)
                rot = v * cos_ref[...] + pltpu.roll(v, HEAD_DIM // 2, 1) * sin_ref[...]
                kv[which] = rot.astype(BF16)
            kv[2] = part(2)
            for b in range(seq // block):
                keys = (b + 1) * block
                sc = lax.dot_general(kv[0, pl.ds(b * block, block)], kv[1, pl.ds(0, keys)], (((1,), (1,)), ((), ())), preferred_element_type=F32)
                sc = sc * HEAD_DIM ** -0.5
                q_pos = b * block + lax.broadcasted_iota(jnp.int32, (block, keys), 0)
                k_pos = lax.broadcasted_iota(jnp.int32, (block, keys), 1)
                sc = jnp.where(q_pos >= k_pos, sc, -1e30)
                e = jnp.exp(sc - jnp.max(sc, axis=-1, keepdims=True))
                prob = (e / jnp.sum(e, axis=-1, keepdims=True)).astype(BF16)
                o = jnp.dot(prob, kv[2, pl.ds(0, keys)], preferred_element_type=F32).astype(BF16)
                for n in range(block // tok):
                    at = (b * (block // tok) + n) * spd + s
                    x2[at, :, pl.ds(2 * c3 + hd * HEAD_DIM, HEAD_DIM)] = o[n * tok : (n + 1) * tok]

    oe = exchange(
        1,
        lambda p: x2.at[pl.ds(p * spd, spd), :, pl.ds(2 * c3, hc)],
        lambda o: x2.at[pl.ds(o * spd, spd), :, pl.ds(2 * c3 + hc, hc)],
    )
    oe.start()
    rings[3].finish()
    g1.drain()
    for k in range(1, tx_count):
        for sl in range(spd):
            for c in (0, 1):
                src, dst, i = qkv_copy(me_tx, k, sl, c, True, me_tx * spd + sl)
                remote(src, dst, qkv_s.at[i], qkv_r.at[i], {"tx": me_tx}).wait_send()
    oe.wait()
    oe.drain()
    r_gate.start(place=False)
    r_up.start(place=False)
    r_down.start()

    def put(off, x, out):
        for c, s, at in pieces(off):
            xp[s, pl.ds(c * q2, q2), col(x * dx, dx)] = out[at : at + q2]

    def o_group(bi):
        off = ORDER[bi]
        stage(x2, off, os_, pl.ds(2 * c3 + hc, hc))

        @pl.loop(0, tx_count)
        def _(x):
            put(off, x, jnp.dot(os_[...], wo[x], preferred_element_type=F32).astype(BF16))

    def weights_1(n):
        if n == 1:
            r_gate.step()
        if n == 3:
            r_up.step()

    sc1 = Scatter(tor, xp, rs_bufs)
    sc1.run(o_group, weights_1)
    sc1.finish(xt, h)
    norm_rows(h, x2.at[tor.me])
    g2 = Gather(tor, x2, gs, gr)
    g2.start()
    sc1.drain()
    xe.drain()

    def mlp_group(off):
        stage(x2, off, xs, pl.ds(0, d))
        width = 256 if fp % 256 == 0 else 128

        @pl.loop(0, fp // width)
        def _(n):
            cols = col(n * width, width)
            gate = jnp.dot(xs[...], wg[:, :, cols].reshape(d, width), preferred_element_type=F32).astype(BF16).astype(F32)
            up = jnp.dot(xs[...], wu[:, :, cols].reshape(d, width), preferred_element_type=F32).astype(BF16).astype(F32)
            act[:, cols] = (gate * jax.nn.sigmoid(gate) * up).astype(BF16)

        @pl.loop(0, tx_count)
        def _(x):
            put(off, x, jnp.dot(act[...], wd[x], preferred_element_type=F32).astype(BF16))

    g2.near()
    r_down.step()
    g2.relay(0)
    r_gate.step2()
    g2.far()
    r_up.step2()
    g2.relay(-1)
    g2.relay(1)
    g2.halves(0)
    r_down.step2()
    r_gate.finish(place=False)
    r_up.finish(place=False)
    r_down.finish()
    mlp_group(0)
    g2.relay(2)
    g2.halves(-1)
    mlp_group(-1)
    g2.halves(1)
    mlp_group(1)
    g2.halves(2)

    def mlp_rest(bi):
        if ORDER[bi] == 2:
            mlp_group(2)

    sc2 = Scatter(tor, xp, rs_bufs)
    sc2.run(mlp_rest, lambda n: None)
    sc2.finish(h, xt)
    ye = exchange(
        2,
        lambda p: xt.at[:, col(p * dx, dx)],
        lambda o: yr.at[pl.ds(pl.multiple_of(o * tok, tok), tok)],
    )
    ye.start()
    g2.drain()
    sc2.drain()
    for r in rings + [r_gate, r_up, r_down]:
        r.drain()
    ye.wait()
    y_ref[...] = yr[...]
    ye.drain()


VMEM_SPEC = pl.BlockSpec(memory_space=pltpu.VMEM)
ANY_SPEC = pl.BlockSpec(memory_space=pl.ANY)


def rotary_tables(seq_len):
    half = HEAD_DIM // 2
    inv_freq = (THETA ** (-2.0 * np.arange(half) / HEAD_DIM)).astype(np.float32)
    angles = np.arange(seq_len, dtype=np.float32)[:, None] * inv_freq[None, :]
    cos_t, sin_t = np.cos(angles), np.sin(angles)
    return np.concatenate([cos_t, cos_t], -1), np.concatenate([-sin_t, sin_t], -1)


def solution(mesh):
    tx_count, n_dev = mesh.shape["tx"], mesh.shape["ty"]
    act_spec = P(("dp", "ty"), None, "tx")
    col_spec = P("tx", "ty")
    row_spec = P("ty", "tx")
    dma = pltpu.SemaphoreType.DMA

    def layer_fn(x_blk, w_q, w_k, w_v, w_o, w_gate, w_up, w_down):
        seq, dx = x_blk.shape[1:]
        hc, f = w_q.shape[1], w_gate.shape[1]
        tok, d = seq // tx_count, dx * tx_count
        fp = -(-f // 128) * 128
        rows = 4 * tok
        cos_t, sin_t = rotary_tables(seq)
        bf = lambda *shape: pltpu.VMEM(shape, BF16)
        scratch = [
            bf(n_dev, tok, d), bf(n_dev, tok, d), bf(tx_count, dx, 3 * hc), bf(tx_count, hc, dx),
            bf(tx_count, dx, fp), bf(tx_count, dx, fp), bf(tx_count, fp, dx),
            bf(rows, d), bf(rows, hc), bf(rows, fp), bf(3, seq, HEAD_DIM), bf(tok, d), bf(tok, d), bf(seq, dx),
            dma((2,)), dma((3, tx_count)), dma((3, tx_count)), dma((2 * n_dev,)), dma((2 * n_dev,)),
            dma((Gather.SEMS,)), dma((Gather.SEMS,)), dma((7 * RING_SEMS,)), dma((7 * RING_SEMS,)),
        ] + Scatter.buffers(tok, d)
        y = pl.pallas_call(
            functools.partial(layer_kernel, tx_count),
            name="layer",
            out_shape=jax.ShapeDtypeStruct((seq, dx), BF16),
            in_specs=[VMEM_SPEC] + [ANY_SPEC] * 7 + [VMEM_SPEC] * 2,
            out_specs=VMEM_SPEC,
            scratch_shapes=scratch,
            compiler_params=pltpu.CompilerParams(collective_id=1, has_side_effects=True, vmem_limit_bytes=67043328),
        )(x_blk[0], w_q, w_k, w_v, w_o, w_gate.T, w_up.T, w_down, cos_t, sin_t)
        return y[None]

    return jax.shard_map(layer_fn, mesh=mesh, in_specs=(act_spec, col_spec, col_spec, col_spec, row_spec, col_spec, col_spec, row_spec), out_specs=act_spec, check_vma=False)
```

time: 367 us -> 262 us (0.71)
  Pallas kernels: 344 us -> 260 us
  between operations: 13.5 us -> 0.01 us
  other arithmetic: 5.69 us -> 0 us
    pallas_call x3 -> x1, Pallas kernels: 344 us -> 260 us  [layer_fn(): pl.pallas_call(functools.partial(layer_kernel, tx_count), name='layer', o...]
    concatenate x3 -> x0, other arithmetic: 4.69 us -> none  [the longest x1 2.24 us: layer_fn(): jnp.concatenate([w_q, w_k, w_v, w_o_rows], axis=1)]
  transfers between devices with their start and end apart: 2 -> 0, of which waited for: 0 -> 0; matrix products, arithmetic and copies ran while one was open for 1% -> 0% of each run, Pallas kernels for 53% -> 0%
where the time goes in v3:
time: 262 us; the launch traced here: 261 us
  Pallas kernels  260 us (99%)
    pallas_call x1, Pallas kernels, layer_fn(): pl.pallas_call(functools.partial(layer_kernel, tx_count), name='layer', o...  260 us

profile of v3, /device:TPU:1, one launch (start us, length us, event | category | flops | bytes accessed | tf_op | source)
XLA Modules:
  0.0 261.4 jit_solution(13135774449795653748)
XLA Ops:
  0.0 259.5 %layer.1 = bf16[512,512]{1,0:T(8,128)(2,1)} custom-call(bf16[512,512]{1,0:T(8,128)(2,1)} %bitcast.7, bf16[512,256]{1,0:T(8,128)(2,1)} %wq_ref.1, bf16[512,256]{1,0:T(8,128)(2,1)} %wk_ref.1, bf16[512,256]{1,0:T(8,128)(2,1)} %wv_ref.1, bf16[256,512]{1,0:T(8,128)(2,1)} %wo_ref.1, bf16[688,512]{1,0:T(8,128)(2,1)} %bitcast.5, bf16[688,512]{1,0:T(8,128)(2,1)} %bitcast.6, ...), custom_call_target="tpu_custom_call" | custom-call | tf_op jit(solution)/shard_map/layer/pallas_call | solution.py:680
  259.5 1.9 copy.12

commit v4 on v3

v4 whole, which is shorter than its diff:
```python
import functools

import numpy as np
import jax
import jax.numpy as jnp
from jax import lax
from jax.experimental import pallas as pl
from jax.experimental.pallas import tpu as pltpu
from jax.sharding import PartitionSpec as P

HEAD_DIM = 128
EPS = 1e-5
THETA = 10000.0
RING = 4
MESH = pl.DeviceIdType.MESH
BF16 = jnp.bfloat16
F32 = jnp.float32
AWAY = (0, -1, 1, 2)


def wrap(v, n):
    return lax.rem(v + 2 * n, n)


class Torus:
    def __init__(self):
        t = lax.axis_index("ty")
        self.me = t
        self.pos = (lax.div(t, RING), lax.rem(t, RING))

    def slot(self, first, a_off, b_off):
        a = wrap(self.pos[first] + a_off, RING)
        b = wrap(self.pos[1 - first] + b_off, RING)
        return a * RING + b if first == 0 else b * RING + a


def entry_barrier(tor, tx_count):
    sem = pltpu.get_barrier_semaphore()
    for first in (0, 1):
        for d in (1, -1):
            pl.semaphore_signal(sem, inc=1, device_id={"ty": tor.slot(first, d, 0)}, device_id_type=MESH)
    me = lax.axis_index("tx")
    for k in range(1, tx_count):
        pl.semaphore_signal(sem, inc=1, device_id={"tx": lax.rem(me + k, tx_count)}, device_id_type=MESH)
    pl.semaphore_wait(sem, 4 + tx_count - 1)


def remote(src, dst, ssem, rsem, device):
    return pltpu.make_async_remote_copy(src_ref=src, dst_ref=dst, send_sem=ssem, recv_sem=rsem, device_id=device, device_id_type=MESH)


class Gather:
    SEMS = 25

    def __init__(self, tor, buf, ssem, rsem):
        self.tor, self.buf, self.ssem, self.rsem = tor, buf, ssem, rsem
        self.q = buf.shape[1] // 4

    def first(self, c):
        return 1 if c == 0 else 0

    def rows(self, c, d, half):
        if not half:
            return pl.ds(c * 2 * self.q, 2 * self.q)
        return pl.ds(c * 2 * self.q + (0 if d == 1 else self.q), self.q)

    def sem(self, c, ph, off, d, half):
        if half:
            return 20 + (0 if ph == 1 else 1 + AWAY.index(off))
        return (0 if ph == 1 else 4 + 4 * AWAY.index(off)) + c * 2 + (0 if d == 1 else 1)

    def copy(self, c, ph, off, d, half, hops):
        first = self.first(c)
        back = -d * hops
        s = self.tor.slot(first, back, 0) if ph == 1 else self.tor.slot(first, off, back)
        to = self.tor.slot(first, d, 0) if ph == 1 else self.tor.slot(first, 0, d)
        view = self.buf.at[s, self.rows(c, d, half)]
        return remote(view, view, self.ssem, self.rsem.at[self.sem(c, ph, off, d, half)], {"ty": to})

    def send(self, c, ph, off, d, half=False):
        self.copy(c, ph, off, d, half, 1 if half else 0).start()

    def recv(self, c, ph, off, d):
        self.copy(c, ph, off, d, False, 1).wait_recv()

    def recv_halves(self, ph, off):
        view = self.buf.at[0]
        remote(view, view, self.ssem, self.rsem.at[self.sem(0, ph, off, 1, True)], {"ty": self.tor.me}).wait_recv()

    def start(self):
        for ph in (1, 2):
            for c in (0, 1):
                for d in (1, -1):
                    self.send(c, ph, 0, d)

    def near(self):
        for d in (1, -1):
            for c in (0, 1):
                self.recv(c, 1, 0, d)
                self.send(c, 1, 0, d, True)

    def spread(self, off):
        for c in (0, 1):
            for d in (1, -1):
                self.send(c, 2, off, d)

    def relay(self, off):
        for d in (1, -1):
            for c in (0, 1):
                self.recv(c, 2, off, d)
                self.send(c, 2, off, d, True)

    def far(self):
        self.recv_halves(1, 0)
        self.spread(2)

    def halves(self, off):
        self.recv_halves(2, off)

    def drain(self):
        view = self.buf.at[pl.ds(0, self.buf.shape[0] - 1)]
        remote(view, view, self.ssem, self.rsem.at[0], {"ty": self.tor.me}).wait_send()


def add_rows(dst, srcs, width=512):
    d = dst.shape[-1]
    width = min(width, d)

    @pl.loop(0, d // width)
    def _(i):
        cols = pl.ds(pl.multiple_of(i * width, width), width)
        tot = srcs[0][:, cols].astype(F32)
        for s in srcs[1:]:
            tot += s[:, cols].astype(F32)
        dst[:, cols] = tot.astype(dst.dtype)


class Scatter:
    SEMS = 30

    @staticmethod
    def buffers(tok, d):
        q = tok // 4
        return [
            pltpu.VMEM((2, 4, 2, q, d), BF16),
            pltpu.VMEM((2, 4, 2, 2 * q, d), BF16),
            pltpu.VMEM((2, 3, 2 * q, d), BF16),
            pltpu.VMEM((2, 2, q, d), BF16),
            pltpu.VMEM((2, 2, 2 * q, d), BF16),
            pltpu.SemaphoreType.DMA,
            pltpu.SemaphoreType.DMA((Scatter.SEMS,)),
        ]

    def __init__(self, tor, part, bufs, order):
        self.tor, self.part, self.order = tor, part, order
        self.h1, self.f1, self.mid, self.h2, self.f2, self.ssem, self.rsem = bufs
        self.q = part.shape[1] // 4

    def copy(self, c, ph, bi, d, kind):
        q, first = self.q, c
        di = 0 if d == 1 else 1
        h = di if kind in (0, 2) else 1 - di
        step = 2 * d if kind == 0 else d
        if ph == 1:
            i = c * 8 + bi * 2 + di if kind == 0 else 16 + c * 4 + bi
            src = self.part.at[self.tor.slot(first, step, self.order[bi]), pl.ds(c * 2 * q + h * q, q)]
            dst = self.h1.at[c, bi, di] if kind == 0 else self.f1.at[c, bi, di, pl.ds(h * q, q)]
            to = self.tor.slot(first, d, 0)
        else:
            i = 24 + c * 2 + di if kind == 0 else 28 + c
            src = self.mid.at[c, self.order.index(2 if kind == 0 else d), pl.ds(h * q, q)]
            dst = self.h2.at[c, di] if kind == 0 else self.f2.at[c, di, pl.ds(h * q, q)]
            to = self.tor.slot(first, 0, d)
        return remote(src, dst, self.ssem, self.rsem.at[i], {"ty": to})

    def all_of(self, view, i):
        remote(view, view, self.ssem, self.rsem.at[i], {"ty": self.tor.me}).wait_recv()

    def issue(self, bi):
        for kind in (0, 1):
            for c in (0, 1):
                for d in (1, -1):
                    self.copy(c, 1, bi, d, kind).start()

    def augment(self, bi):
        q = self.q
        for c in (0, 1):
            for d in (1, -1):
                di = 0 if d == 1 else 1
                self.copy(c, 1, bi, d, 0).wait_recv()
                mine = self.part.at[self.tor.slot(c, d, self.order[bi]), pl.ds(c * 2 * q + di * q, q)]
                add_rows(mine, [mine, self.h1.at[c, bi, di]])
                self.copy(c, 1, bi, d, 2).start()

    def arrived(self, bi):
        q = self.q
        for c in (0, 1):
            self.all_of(self.f1.at[c, bi], 16 + c * 4 + bi)
            off = self.order[bi]
            if off == 0:
                continue
            own = self.part.at[self.tor.slot(c, 0, off), pl.ds(c * 2 * q, 2 * q)]
            add_rows(self.mid.at[c, bi], [own, self.f1.at[c, bi, 0], self.f1.at[c, bi, 1]])
            if off == 2:
                for d in (1, -1):
                    self.copy(c, 2, 0, d, 0).start()
            else:
                self.copy(c, 2, 0, off, 1).start()

    def augment2(self, d):
        q = self.q
        di = 0 if d == 1 else 1
        for c in (0, 1):
            self.copy(c, 2, 0, d, 0).wait_recv()
            mine = self.mid.at[c, self.order.index(d), pl.ds(di * q, q)]
            add_rows(mine, [mine, self.h2.at[c, di]])
            self.copy(c, 2, 0, d, 2).start()

    def last(self):
        for c in (0, 1):
            self.all_of(self.f2.at[c], 28 + c)

    def finish(self, resid, out):
        q, d = self.q, out.shape[-1]
        width = min(512, d)
        for c in (0, 1):
            rows = pl.ds(c * 2 * q, 2 * q)

            @pl.loop(0, d // width)
            def _(i):
                cols = pl.ds(pl.multiple_of(i * width, width), width)
                tot = self.part[self.tor.me, rows, cols].astype(F32)
                for di in (0, 1):
                    tot += self.f1[c, self.order.index(0), di, :, cols].astype(F32)
                for di in (0, 1):
                    tot += self.f2[c, di, :, cols].astype(F32)
                tot = tot.astype(BF16).astype(F32)
                out[rows, cols] = (resid[rows, cols].astype(F32) + tot).astype(BF16)

    def drain(self):
        view = self.part.at[pl.ds(0, self.part.shape[0] - 1)]
        remote(view, view, self.ssem, self.rsem.at[0], {"ty": self.tor.me}).wait_send()


class Exchange:
    def __init__(self, tx_count, src, dst, whole, ssem, rsem):
        self.n, self.src, self.dst, self.whole, self.ssem, self.rsem = tx_count, src, dst, whole, ssem, rsem
        self.me = lax.axis_index("tx")

    def start(self):
        for k in range(1, self.n):
            p = lax.rem(self.me + k, self.n)
            remote(self.src(p), self.dst(self.me), self.ssem, self.rsem, {"tx": p}).start()
        pltpu.make_async_copy(self.src(self.me), self.dst(self.me), self.rsem).start()

    def wait(self):
        view = self.whole(self.n)
        remote(view, view, self.ssem, self.rsem, {"tx": self.me}).wait_recv()

    def drain(self):
        view = self.whole(self.n - 1)
        remote(view, view, self.ssem, self.rsem, {"tx": self.me}).wait_send()


def norm_rows(src, dst):
    tok, d = src.shape
    step = 16

    @pl.loop(0, tok // step)
    def _(i):
        rows = pl.ds(pl.multiple_of(i * step, step), step)
        v = src[rows, :].astype(F32)
        mean = jnp.sum(v, axis=-1, keepdims=True) * (1.0 / d)
        var = jnp.sum(v * v, axis=-1, keepdims=True) * (1.0 / d) - mean * mean
        dst[rows, :] = ((v - mean) * lax.rsqrt(var + EPS)).astype(BF16)


class Ring:
    SEMS = 5

    def __init__(self, tx_count, rows, src, slot, whole, ssem, rsem):
        self.nx, self.rows, self.src, self.slot, self.whole, self.ssem, self.rsem = tx_count // 2, rows, src, slot, whole, ssem, rsem
        me = lax.axis_index("tx")
        self.me, self.x, self.core = me, lax.div(me, 2), lax.rem(me, 2)
        self.split = (rows // 2 + 15) // 16 * 16

    def tx(self, dx, other=False):
        return wrap(self.x + dx, self.nx) * 2 + (1 - self.core if other else self.core)

    def half(self, view, d):
        return view.at[pl.ds(0, self.split)] if d == 1 else view.at[pl.ds(self.split, self.rows - self.split)]

    def copy(self, i, src, dst, to):
        return remote(src, dst, self.ssem, self.rsem.at[i], {"tx": to})

    def pass_on(self, d, recv=False):
        view = self.slot(self.tx(-d if recv else 0))
        return self.copy(0 if d == 1 else 1, view if recv else self.src, view, self.tx(d))

    def relay(self, d, recv=False):
        view = self.half(self.slot(self.tx(-2 * d if recv else -d)), d)
        return self.copy(2 if d == 1 else 3, view, view, self.tx(d))

    def across(self, which, recv=False):
        view = self.slot(self.tx(which, recv))
        if abs(which) == 2:
            view = self.half(view, which // 2)
        src = self.src if which == 0 and not recv else view
        return self.copy(4, src, view, self.tx(0, True))

    def all_across(self):
        return (0, 1, -1, 2, -2) if self.nx > 1 else (0,)

    def own(self):
        return pltpu.make_async_copy(self.src, self.slot(self.me), self.rsem.at[4])

    def start(self, place=True):
        if self.nx > 1:
            for d in (1, -1):
                self.pass_on(d).start()
        self.across(0).start()
        if place:
            self.own().start()

    def step(self):
        if self.nx > 1:
            for d in (1, -1):
                self.pass_on(d, True).wait_recv()
                self.relay(d).start()
                self.across(-d).start()

    def step2(self):
        if self.nx > 1:
            for d in (1, -1):
                self.relay(d, True).wait_recv()
                self.across(2 * d).start()

    def finish(self, place=True):
        view = self.whole(self.nx + (1 if place else 0))
        remote(view, view, self.ssem, self.rsem.at[4], {"tx": self.me}).wait_recv()

    def drain(self):
        view = self.whole(2 * self.nx - 1)
        remote(view, view, self.ssem, self.rsem.at[4], {"tx": self.me}).wait_send()


def layer_kernel(tx_count, x_ref, wq_ref, wk_ref, wv_ref, wo_ref, wg_ref, wu_ref, wd_ref, cos_hbm, sin_hbm, y_ref,
                 xp, x2, wqkv, wo, wg, wu, wd, xs, os_, act, kv, xt, h, yr, cos_ref, sin_ref,
                 load_sem, a2a_s, a2a_r, qkv_s, qkv_r, gs, gr, ws, wr, *rs_bufs):
    n_dev, tok, d = xp.shape
    dx = x_ref.shape[1]
    hc = wq_ref.shape[1]
    f, fp = wg_ref.shape[0], wg.shape[2]
    seq = tok * tx_count
    spd = n_dev // tx_count
    heads = hc // HEAD_DIM
    q2 = tok // 2
    c3 = 3 * hc
    tor = Torus()
    me_tx = lax.axis_index("tx")

    def exchange(i, src, dst, whole):
        return Exchange(tx_count, src, dst, whole, a2a_s.at[i], a2a_r.at[i])

    def col(start, width):
        return pl.ds(pl.multiple_of(start, width), width)

    def ring(i, src, buf, inner):
        return Ring(tx_count, src.shape[0], src, lambda o: buf.at[(o, *inner)], lambda n: buf.at[(pl.ds(0, n), *inner)], ws.at[i], wr.at[i])

    every = pl.ds(0, dx)
    rings = [ring(i, src, wqkv, (every, pl.ds(i * hc, hc))) for i, src in enumerate((wq_ref, wk_ref, wv_ref))]
    r_o = ring(3, wo_ref, wo, ())
    r_gate = ring(4, wg.at[me_tx], wg, ())
    r_up = ring(5, wu.at[me_tx], wu, ())
    r_down = ring(6, wd_ref, wd, (pl.ds(0, f),))

    x_in = pltpu.make_async_copy(x_ref, yr, load_sem.at[2])
    x_in.start()
    raw = [pltpu.make_async_copy(src, wd.at[i, pl.ds(0, f)], load_sem.at[i]) for i, src in enumerate((wg_ref, wu_ref))]
    raw += [pltpu.make_async_copy(cos_hbm, cos_ref, load_sem.at[3]), pltpu.make_async_copy(sin_hbm, sin_ref, load_sem.at[4])]
    for cp in raw:
        cp.start()
    entry_barrier(tor, tx_count)
    x_in.wait()
    xe = exchange(
        0,
        lambda p: yr.at[pl.ds(pl.multiple_of(p * tok, tok), tok)],
        lambda o: xt.at[:, col(o * dx, dx)],
        lambda n: yr.at[pl.ds(0, n * tok)],
    )
    xe.start()
    if fp > f:
        wd[:, pl.ds(f, fp - f), :] = jnp.zeros((tx_count, fp - f, dx), BF16)
    xe.wait()
    norm_rows(xt, xp.at[tor.me])
    g1 = Gather(tor, xp, gs, gr)
    g1.start()
    for r in rings:
        r.start()
    for cp in raw:
        cp.wait()
    for i, dst in enumerate((wg, wu)):
        for j in range(fp // 128):
            dst[me_tx, :, pl.ds(j * 128, 128)] = wd[i, pl.ds(j * 128, 128), :].T

    def pieces(off):
        return [(c, tor.slot(1 - c, off, n), (c * 4 + n) * q2) for c in (0, 1) for n in range(RING)]

    def stage(src, off, dst, cols):
        for c, s, at in pieces(off):
            dst[pl.ds(at, q2), :] = src[s, pl.ds(c * q2, q2), cols]

    def qkv_group(off):
        stage(xp, off, xs, pl.ds(0, d))

        @pl.loop(0, 3)
        def _(n):
            cols = col(n * hc, hc)
            out = jnp.dot(xs[...], wqkv[:, :, cols].reshape(d, hc), preferred_element_type=F32).astype(BF16)
            for c, s, at in pieces(off):
                x2[s, pl.ds(c * q2, q2), cols] = out[at : at + q2]

        for c, s, _ in pieces(off):
            p, sl = lax.div(s, spd), lax.rem(s, spd)
            rows = pl.ds(c * q2, q2)
            src = x2.at[s, rows, pl.ds(0, c3)]
            dst = x2.at[sl * tx_count + me_tx, rows, pl.ds(c3, c3)]

            @pl.when(p == me_tx)
            def _():
                pltpu.make_async_copy(src, dst, qkv_r.at[sl]).start()

            @pl.when(p != me_tx)
            def _():
                remote(src, dst, qkv_s, qkv_r.at[sl], {"tx": p}).start()

    xe.drain()
    wq_r, wk_r, wv_r = rings
    g1.near()
    wq_r.step()
    g1.relay(0)
    g1.spread(-1)
    g1.spread(1)
    wk_r.step()
    wv_r.step()
    g1.halves(0)
    wq_r.step2()
    wk_r.step2()
    g1.relay(-1)
    g1.far()
    wv_r.step2()
    g1.relay(1)
    for r in rings:
        r.finish()
    qkv_group(0)
    g1.halves(-1)
    qkv_group(-1)
    g1.relay(2)
    g1.halves(1)
    qkv_group(1)
    g1.halves(2)
    qkv_group(2)

    block = min(seq, 128)
    sends = []
    for s in range(spd):
        view = x2.at[pl.ds(s * tx_count, tx_count), :, pl.ds(c3, c3)]
        remote(view, view, qkv_s, qkv_r.at[s], {"tx": me_tx}).wait_recv()
        if s == spd - 1:
            r_o.start()

        @pl.loop(0, heads)
        def _(hd):
            def part(which):
                return x2[pl.ds(s * tx_count, tx_count), :, col(c3 + which * hc + hd * HEAD_DIM, HEAD_DIM)].reshape(seq, HEAD_DIM)

            for which in (0, 1):
                v = part(which).astype(F32)
                rot = v * cos_ref[...] + pltpu.roll(v, HEAD_DIM // 2, 1) * sin_ref[...]
                kv[which] = rot.astype(BF16)
            kv[2] = part(2)
            for b in range(seq // block):
                keys = (b + 1) * block
                sc = lax.dot_general(kv[0, pl.ds(b * block, block)], kv[1, pl.ds(0, keys)], (((1,), (1,)), ((), ())), preferred_element_type=F32)
                sc = sc * HEAD_DIM ** -0.5
                q_pos = b * block + lax.broadcasted_iota(jnp.int32, (block, keys), 0)
                k_pos = lax.broadcasted_iota(jnp.int32, (block, keys), 1)
                sc = jnp.where(q_pos >= k_pos, sc, -1e30)
                e = jnp.exp(sc - jnp.max(sc, axis=-1, keepdims=True))
                prob = (e / jnp.sum(e, axis=-1, keepdims=True)).astype(BF16)
                o = jnp.dot(prob, kv[2, pl.ds(0, keys)], preferred_element_type=F32).astype(BF16)
                for n in range(block // tok):
                    at = (b * (block // tok) + n) * spd + s
                    x2[at, :, col(2 * c3 + hd * HEAD_DIM, HEAD_DIM)] = o[n * tok : (n + 1) * tok]

        oe = exchange(
            1 + s,
            lambda p, s=s: x2.at[p * spd + s, :, pl.ds(2 * c3, hc)],
            lambda o, s=s: x2.at[o * spd + s, :, pl.ds(2 * c3 + hc, hc)],
            lambda n: x2.at[pl.ds(0, n), :, pl.ds(2 * c3, hc)],
        )
        oe.start()
        sends.append(oe)

    r_o.step()
    g1.drain()
    view = x2.at[pl.ds(0, (tx_count - 1) * spd), :, pl.ds(0, c3)]
    remote(view, view, qkv_s, qkv_r.at[0], {"tx": me_tx}).wait_send()
    for oe in sends:
        oe.wait()
        oe.drain()
    r_o.step2()
    r_gate.start(place=False)
    r_up.start(place=False)
    r_down.start()
    r_o.finish()

    def put(off, x, out):
        for c, s, at in pieces(off):
            xp[s, pl.ds(c * q2, q2), col(x * dx, dx)] = out[at : at + q2]

    def o_group(off):
        stage(x2, off, os_, pl.ds(2 * c3 + hc, hc))

        @pl.loop(0, tx_count)
        def _(x):
            put(off, x, jnp.dot(os_[...], wo[x], preferred_element_type=F32).astype(BF16))

    order = (2, -1, 1, 0)
    sc1 = Scatter(tor, xp, rs_bufs, order)
    o_group(order[0])
    sc1.issue(0)
    o_group(order[1])
    sc1.issue(1)
    o_group(order[2])
    sc1.augment(0)
    sc1.issue(2)
    o_group(order[3])
    sc1.augment(1)
    sc1.issue(3)
    sc1.arrived(0)
    r_gate.step()
    sc1.augment(2)
    sc1.arrived(1)
    sc1.augment2(-1)
    sc1.augment(3)
    sc1.arrived(2)
    sc1.augment2(1)
    r_up.step()
    sc1.arrived(3)
    sc1.last()
    sc1.finish(xt, h)
    norm_rows(h, x2.at[tor.me])
    g2 = Gather(tor, x2, gs, gr)
    g2.start()
    sc1.drain()

    def mlp_group(off, between):
        stage(x2, off, xs, pl.ds(0, d))
        width = 256 if fp % 256 == 0 else 128

        @pl.loop(0, fp // width)
        def _(n):
            cols = col(n * width, width)
            gate = jnp.dot(xs[...], wg[:, :, cols].reshape(d, width), preferred_element_type=F32).astype(BF16).astype(F32)
            up = jnp.dot(xs[...], wu[:, :, cols].reshape(d, width), preferred_element_type=F32).astype(BF16).astype(F32)
            act[:, cols] = (gate * jax.nn.sigmoid(gate) * up).astype(BF16)

        between()

        @pl.loop(0, tx_count)
        def _(x):
            put(off, x, jnp.dot(act[...], wd[x], preferred_element_type=F32).astype(BF16))

    sc2 = Scatter(tor, xp, rs_bufs, (-1, 1, 2, 0))
    g2.near()
    r_down.step()
    g2.relay(0)
    g2.spread(-1)
    g2.spread(1)
    r_gate.step2()
    r_up.step2()
    g2.halves(0)
    r_gate.finish(place=False)
    r_up.finish(place=False)

    def rest():
        g2.relay(-1)
        g2.far()
        r_down.step2()
        r_down.finish()

    mlp_group(0, rest)
    g2.relay(1)
    g2.halves(-1)
    mlp_group(-1, lambda: g2.relay(2))
    sc2.issue(0)
    g2.halves(1)
    mlp_group(1, lambda: None)
    sc2.issue(1)
    g2.halves(2)
    mlp_group(2, lambda: None)
    sc2.issue(2)
    sc2.augment(0)
    sc2.augment(1)
    sc2.issue(3)
    sc2.arrived(0)
    sc2.augment(2)
    sc2.arrived(1)
    sc2.arrived(2)
    sc2.augment(3)
    sc2.augment2(-1)
    sc2.augment2(1)
    sc2.arrived(3)
    sc2.last()
    sc2.finish(h, xt)
    ye = exchange(
        1 + spd,
        lambda p: xt.at[:, col(p * dx, dx)],
        lambda o: yr.at[pl.ds(pl.multiple_of(o * tok, tok), tok)],
        lambda n: yr.at[pl.ds(0, n * tok)],
    )
    ye.start()
    g2.drain()
    sc2.drain()
    for r in rings + [r_o, r_gate, r_up, r_down]:
        r.drain()
    ye.wait()
    out = pltpu.make_async_copy(yr, y_ref, load_sem.at[0])
    out.start()
    ye.drain()
    out.wait()


ANY_SPEC = pl.BlockSpec(memory_space=pl.ANY)


def rotary_tables(seq_len):
    half = HEAD_DIM // 2
    inv_freq = (THETA ** (-2.0 * np.arange(half) / HEAD_DIM)).astype(np.float32)
    angles = np.arange(seq_len, dtype=np.float32)[:, None] * inv_freq[None, :]
    cos_t, sin_t = np.cos(angles), np.sin(angles)
    return np.concatenate([cos_t, cos_t], -1), np.concatenate([-sin_t, sin_t], -1)


def solution(mesh):
    tx_count, n_dev = mesh.shape["tx"], mesh.shape["ty"]
    act_spec = P(("dp", "ty"), None, "tx")
    col_spec = P("tx", "ty")
    row_spec = P("ty", "tx")
    dma = pltpu.SemaphoreType.DMA

    def layer_fn(x_blk, w_q, w_k, w_v, w_o, w_gate, w_up, w_down):
        seq, dx = x_blk.shape[1:]
        hc, f = w_q.shape[1], w_gate.shape[1]
        tok, d = seq // tx_count, dx * tx_count
        fp = -(-f // 128) * 128
        rows, spd = 4 * tok, n_dev // tx_count
        cos_t, sin_t = rotary_tables(seq)
        bf = lambda *shape: pltpu.VMEM(shape, BF16)
        scratch = [
            bf(n_dev, tok, d), bf(n_dev, tok, d), bf(tx_count, dx, 3 * hc), bf(tx_count, hc, dx),
            bf(tx_count, dx, fp), bf(tx_count, dx, fp), bf(tx_count, fp, dx),
            bf(rows, d), bf(rows, hc), bf(rows, fp), bf(3, seq, HEAD_DIM), bf(tok, d), bf(tok, d), bf(seq, dx),
            pltpu.VMEM((seq, HEAD_DIM), F32), pltpu.VMEM((seq, HEAD_DIM), F32),
            dma((5,)), dma((spd + 2,)), dma((spd + 2,)), dma, dma((spd,)),
            dma, dma((Gather.SEMS,)), dma((7,)), dma((7, Ring.SEMS)),
        ] + Scatter.buffers(tok, d)
        y = pl.pallas_call(
            functools.partial(layer_kernel, tx_count),
            name="layer",
            out_shape=jax.ShapeDtypeStruct((seq, dx), BF16),
            in_specs=[ANY_SPEC] * 10,
            out_specs=ANY_SPEC,
            scratch_shapes=scratch,
            compiler_params=pltpu.CompilerParams(collective_id=1, has_side_effects=True, vmem_limit_bytes=67043328),
        )(x_blk[0], w_q, w_k, w_v, w_o, w_gate.T, w_up.T, w_down, cos_t, sin_t)
        return y[None]

    return jax.shard_map(layer_fn, mesh=mesh, in_specs=(act_spec, col_spec, col_spec, col_spec, row_spec, col_spec, col_spec, row_spec), out_specs=act_spec, check_vma=False)
```

time: 262 us -> 245 us (0.935)
  Pallas kernels: 260 us -> 243 us
    pallas_call x1, Pallas kernels: 260 us -> 243 us  [layer_fn(): pl.pallas_call(functools.partial(layer_kernel, tx_count), name='layer', o...]
where the time goes in v4:
time: 245 us
  Pallas kernels  243 us (99%)
    pallas_call x1, Pallas kernels, layer_fn(): pl.pallas_call(functools.partial(layer_kernel, tx_count), name='layer', o...  243 us

profile of v4, /device:TPU:1, one launch (start us, length us, event | category | flops | bytes accessed | tf_op | source)
XLA Modules:
  0.0 244.9 jit_solution(9952909160849217682)
XLA Ops:
  0.0 243.0 %layer.1 = bf16[512,512]{1,0:T(8,128)(2,1)} custom-call(bf16[512,512]{1,0:T(8,128)(2,1)} %bitcast.7, bf16[512,256]{1,0:T(8,128)(2,1)} %wq_ref.1, bf16[512,256]{1,0:T(8,128)(2,1)} %wk_ref.1, bf16[512,256]{1,0:T(8,128)(2,1)} %wv_ref.1, bf16[256,512]{1,0:T(8,128)(2,1)} %wo_ref.1, bf16[688,512]{1,0:T(8,128)(2,1)} %bitcast.5, bf16[688,512]{1,0:T(8,128)(2,1)} %bitcast.6, ...), custom_call_target="tpu_custom_call" | custom-call | tf_op jit(solution)/shard_map/layer/pallas_call | solution.py:670
  243.0 1.9 copy.12

commit v5 on v4

--- a/solution.py
+++ b/solution.py
@@ -346,7 +346,7 @@
 
 def layer_kernel(tx_count, x_ref, wq_ref, wk_ref, wv_ref, wo_ref, wg_ref, wu_ref, wd_ref, cos_hbm, sin_hbm, y_ref,
                  xp, x2, wqkv, wo, wg, wu, wd, xs, os_, act, kv, xt, h, yr, cos_ref, sin_ref,
-                 load_sem, a2a_s, a2a_r, qkv_s, qkv_r, gs, gr, ws, wr, *rs_bufs):
+                 load_sem, a2a_s, a2a_r, qkv_s, qkv_r, via_s, via_r, gs, gr, ws, wr, *rs_bufs):
     n_dev, tok, d = xp.shape
     dx = x_ref.shape[1]
     hc = wq_ref.shape[1]
@@ -411,6 +411,14 @@
         for c, s, at in pieces(off):
             dst[pl.ds(at, q2), :] = src[s, pl.ds(c * q2, q2), cols]
 
+    detours = tx_count == 8
+    x_pos = lax.div(me_tx, 2)
+    edge = (x_pos == 0) | (x_pos == 3)
+    opposite = jnp.where(x_pos == 0, 2, 1)
+    inner = jnp.where(x_pos == 0, 1, 2)
+    over = (3 - x_pos) * 2 + lax.rem(me_tx, 2)
+    via = pl.ds(2 * c3 + 2 * hc, c3)
+
     def qkv_group(off):
         stage(xp, off, xs, pl.ds(0, d))
 
@@ -427,13 +435,52 @@
             src = x2.at[s, rows, pl.ds(0, c3)]
             dst = x2.at[sl * tx_count + me_tx, rows, pl.ds(c3, c3)]
 
+            detour = (p != p) if off == 2 or not detours else edge & (lax.div(p, 2) == opposite)
+
             @pl.when(p == me_tx)
             def _():
                 pltpu.make_async_copy(src, dst, qkv_r.at[sl]).start()
 
-            @pl.when(p != me_tx)
+            @pl.when(detour)
+            def _():
+                remote(src, x2.at[s, rows, via], qkv_s, via_r.at[2 * AWAY.index(off) + c], {"tx": over}).start()
+
+            @pl.when((p != me_tx) & jnp.logical_not(detour))
             def _():
                 remote(src, dst, qkv_s, qkv_r.at[sl], {"tx": p}).start()
+
+    def detour_rows(off, c):
+        rows = pl.ds(c * q2, q2)
+        return [(s, rows) for s in ([inner * RING + wrap(tor.pos[1] + off, RING)] if c == 0 else [inner * RING + y for y in range(RING)])]
+
+    def pass_detour(off):
+        if not detours:
+            return
+        for c in (0, 1):
+
+            @pl.when(edge if c == 0 else edge & (wrap(tor.pos[0] + off, RING) == inner))
+            def _():
+                for s, rows in detour_rows(off, c):
+                    view = x2.at[s, rows, via]
+                    if c == 0:
+                        remote(view, view, via_s, via_r.at[2 * AWAY.index(off) + c], {"tx": me_tx}).wait_recv()
+                if c == 1:
+                    view = x2.at[pl.ds(inner * RING, 2), :, via]
+                    remote(view, view, via_s, via_r.at[2 * AWAY.index(off) + c], {"tx": me_tx}).wait_recv()
+                for s, rows in detour_rows(off, c):
+                    p, sl = lax.div(s, spd), lax.rem(s, spd)
+                    remote(x2.at[s, rows, via], x2.at[sl * tx_count + over, rows, pl.ds(c3, c3)], via_s, qkv_r.at[sl], {"tx": p}).start()
+
+    def drain_detours():
+        if not detours:
+            return
+        for off in (0, -1, 1):
+            for c in (0, 1):
+
+                @pl.when(edge if c == 0 else edge & (wrap(tor.pos[0] + off, RING) == inner))
+                def _():
+                    view = x2.at[0, pl.ds(0, q2), via] if c == 0 else x2.at[pl.ds(0, 2), :, via]
+                    remote(view, view, via_s, via_r.at[0], {"tx": me_tx}).wait_send()
 
     xe.drain()
     wq_r, wk_r, wv_r = rings
@@ -444,31 +491,35 @@
     g1.spread(1)
     wk_r.step()
     wv_r.step()
+    r_o.start()
     g1.halves(0)
     wq_r.step2()
     wk_r.step2()
     g1.relay(-1)
-    g1.far()
     wv_r.step2()
-    g1.relay(1)
     for r in rings:
         r.finish()
     qkv_group(0)
+    g1.relay(1)
+    g1.far()
+    r_o.step()
     g1.halves(-1)
     qkv_group(-1)
-    g1.relay(2)
     g1.halves(1)
     qkv_group(1)
+    pass_detour(0)
+    g1.relay(2)
+    r_o.step2()
+    pass_detour(-1)
     g1.halves(2)
     qkv_group(2)
+    pass_detour(1)
 
     block = min(seq, 128)
     sends = []
     for s in range(spd):
         view = x2.at[pl.ds(s * tx_count, tx_count), :, pl.ds(c3, c3)]
         remote(view, view, qkv_s, qkv_r.at[s], {"tx": me_tx}).wait_recv()
-        if s == spd - 1:
-            r_o.start()
 
         @pl.loop(0, heads)
         def _(hd):
@@ -503,14 +554,13 @@
         oe.start()
         sends.append(oe)
 
-    r_o.step()
     g1.drain()
+    drain_detours()
     view = x2.at[pl.ds(0, (tx_count - 1) * spd), :, pl.ds(0, c3)]
     remote(view, view, qkv_s, qkv_r.at[0], {"tx": me_tx}).wait_send()
     for oe in sends:
         oe.wait()
         oe.drain()
-    r_o.step2()
     r_gate.start(place=False)
     r_up.start(place=False)
     r_down.start()
@@ -664,7 +714,7 @@
             bf(tx_count, dx, fp), bf(tx_count, dx, fp), bf(tx_count, fp, dx),
             bf(rows, d), bf(rows, hc), bf(rows, fp), bf(3, seq, HEAD_DIM), bf(tok, d), bf(tok, d), bf(seq, dx),
             pltpu.VMEM((seq, HEAD_DIM), F32), pltpu.VMEM((seq, HEAD_DIM), F32),
-            dma((5,)), dma((spd + 2,)), dma((spd + 2,)), dma, dma((spd,)),
+            dma((5,)), dma((spd + 2,)), dma((spd + 2,)), dma, dma((spd,)), dma, dma((6,)),
             dma, dma((Gather.SEMS,)), dma((7,)), dma((7, Ring.SEMS)),
         ] + Scatter.buffers(tok, d)
         y = pl.pallas_call(

time: 245 us -> 248 us (1.012)
  Pallas kernels: 243 us -> 246 us
    pallas_call x1, Pallas kernels: 243 us -> 246 us  [layer_fn(): pl.pallas_call(functools.partial(layer_kernel, tx_count), name='layer', o...]
where the time goes in v5:
time: 248 us
  Pallas kernels  246 us (99%)
    pallas_call x1, Pallas kernels, layer_fn(): pl.pallas_call(functools.partial(layer_kernel, tx_count), name='layer', o...  246 us

profile of v5, /device:TPU:1, one launch (start us, length us, event | category | flops | bytes accessed | tf_op | source)
XLA Modules:
  0.0 248.3 jit_solution(6793450361616891238)
XLA Ops:
  0.0 246.4 %layer.1 = bf16[512,512]{1,0:T(8,128)(2,1)} custom-call(bf16[512,512]{1,0:T(8,128)(2,1)} %bitcast.7, bf16[512,256]{1,0:T(8,128)(2,1)} %wq_ref.1, bf16[512,256]{1,0:T(8,128)(2,1)} %wk_ref.1, bf16[512,256]{1,0:T(8,128)(2,1)} %wv_ref.1, bf16[256,512]{1,0:T(8,128)(2,1)} %wo_ref.1, bf16[688,512]{1,0:T(8,128)(2,1)} %bitcast.5, bf16[688,512]{1,0:T(8,128)(2,1)} %bitcast.6, ...), custom_call_target="tpu_custom_call" | custom-call | tf_op jit(solution)/shard_map/layer/pallas_call | solution.py:720
  246.4 1.9 copy.12

commit v6 on v5

--- a/solution.py
+++ b/solution.py
@@ -12,10 +12,16 @@
 EPS = 1e-5
 THETA = 10000.0
 RING = 4
+BOTH = (0, 1)
+DIRS = (1, -1)
 MESH = pl.DeviceIdType.MESH
 BF16 = jnp.bfloat16
 F32 = jnp.float32
 AWAY = (0, -1, 1, 2)
+
+
+def nothing():
+    pass
 
 
 def wrap(v, n):
@@ -37,7 +43,7 @@
 def entry_barrier(tor, tx_count):
     sem = pltpu.get_barrier_semaphore()
     for first in (0, 1):
-        for d in (1, -1):
+        for d in DIRS:
             pl.semaphore_signal(sem, inc=1, device_id={"ty": tor.slot(first, d, 0)}, device_id_type=MESH)
     me = lax.axis_index("tx")
     for k in range(1, tx_count):
@@ -89,24 +95,24 @@
 
     def start(self):
         for ph in (1, 2):
-            for c in (0, 1):
-                for d in (1, -1):
+            for c in BOTH:
+                for d in DIRS:
                     self.send(c, ph, 0, d)
 
     def near(self):
-        for d in (1, -1):
-            for c in (0, 1):
+        for d in DIRS:
+            for c in BOTH:
                 self.recv(c, 1, 0, d)
                 self.send(c, 1, 0, d, True)
 
     def spread(self, off):
-        for c in (0, 1):
-            for d in (1, -1):
+        for c in BOTH:
+            for d in DIRS:
                 self.send(c, 2, off, d)
 
     def relay(self, off):
-        for d in (1, -1):
-            for c in (0, 1):
+        for d in DIRS:
+            for c in BOTH:
                 self.recv(c, 2, off, d)
                 self.send(c, 2, off, d, True)
 
@@ -177,15 +183,15 @@
         remote(view, view, self.ssem, self.rsem.at[i], {"ty": self.tor.me}).wait_recv()
 
     def issue(self, bi):
-        for kind in (0, 1):
-            for c in (0, 1):
-                for d in (1, -1):
+        for kind in BOTH:
+            for c in BOTH:
+                for d in DIRS:
                     self.copy(c, 1, bi, d, kind).start()
 
     def augment(self, bi):
         q = self.q
-        for c in (0, 1):
-            for d in (1, -1):
+        for c in BOTH:
+            for d in DIRS:
                 di = 0 if d == 1 else 1
                 self.copy(c, 1, bi, d, 0).wait_recv()
                 mine = self.part.at[self.tor.slot(c, d, self.order[bi]), pl.ds(c * 2 * q + di * q, q)]
@@ -194,7 +200,7 @@
 
     def arrived(self, bi):
         q = self.q
-        for c in (0, 1):
+        for c in BOTH:
             self.all_of(self.f1.at[c, bi], 16 + c * 4 + bi)
             off = self.order[bi]
             if off == 0:
@@ -202,7 +208,7 @@
             own = self.part.at[self.tor.slot(c, 0, off), pl.ds(c * 2 * q, 2 * q)]
             add_rows(self.mid.at[c, bi], [own, self.f1.at[c, bi, 0], self.f1.at[c, bi, 1]])
             if off == 2:
-                for d in (1, -1):
+                for d in DIRS:
                     self.copy(c, 2, 0, d, 0).start()
             else:
                 self.copy(c, 2, 0, off, 1).start()
@@ -210,29 +216,29 @@
     def augment2(self, d):
         q = self.q
         di = 0 if d == 1 else 1
-        for c in (0, 1):
+        for c in BOTH:
             self.copy(c, 2, 0, d, 0).wait_recv()
             mine = self.mid.at[c, self.order.index(d), pl.ds(di * q, q)]
             add_rows(mine, [mine, self.h2.at[c, di]])
             self.copy(c, 2, 0, d, 2).start()
 
     def last(self):
-        for c in (0, 1):
+        for c in BOTH:
             self.all_of(self.f2.at[c], 28 + c)
 
     def finish(self, resid, out):
         q, d = self.q, out.shape[-1]
         width = min(512, d)
-        for c in (0, 1):
+        for c in BOTH:
             rows = pl.ds(c * 2 * q, 2 * q)
 
             @pl.loop(0, d // width)
             def _(i):
                 cols = pl.ds(pl.multiple_of(i * width, width), width)
                 tot = self.part[self.tor.me, rows, cols].astype(F32)
-                for di in (0, 1):
+                for di in BOTH:
                     tot += self.f1[c, self.order.index(0), di, :, cols].astype(F32)
-                for di in (0, 1):
+                for di in BOTH:
                     tot += self.f2[c, di, :, cols].astype(F32)
                 tot = tot.astype(BF16).astype(F32)
                 out[rows, cols] = (resid[rows, cols].astype(F32) + tot).astype(BF16)
@@ -316,7 +322,7 @@
 
     def start(self, place=True):
         if self.nx > 1:
-            for d in (1, -1):
+            for d in DIRS:
                 self.pass_on(d).start()
         self.across(0).start()
         if place:
@@ -324,14 +330,14 @@
 
     def step(self):
         if self.nx > 1:
-            for d in (1, -1):
+            for d in DIRS:
                 self.pass_on(d, True).wait_recv()
                 self.relay(d).start()
                 self.across(-d).start()
 
     def step2(self):
         if self.nx > 1:
-            for d in (1, -1):
+            for d in DIRS:
                 self.relay(d, True).wait_recv()
                 self.across(2 * d).start()
 
@@ -405,7 +411,7 @@
             dst[me_tx, :, pl.ds(j * 128, 128)] = wd[i, pl.ds(j * 128, 128), :].T
 
     def pieces(off):
-        return [(c, tor.slot(1 - c, off, n), (c * 4 + n) * q2) for c in (0, 1) for n in range(RING)]
+        return [(c, tor.slot(1 - c, off, n), (c * 4 + n) * q2) for c in BOTH for n in range(RING)]
 
     def stage(src, off, dst, cols):
         for c, s, at in pieces(off):
@@ -435,7 +441,7 @@
             src = x2.at[s, rows, pl.ds(0, c3)]
             dst = x2.at[sl * tx_count + me_tx, rows, pl.ds(c3, c3)]
 
-            detour = (p != p) if off == 2 or not detours else edge & (lax.div(p, 2) == opposite)
+            detour = (p != p) if off > 0 or not detours else edge & (lax.div(p, 2) == opposite)
 
             @pl.when(p == me_tx)
             def _():
@@ -456,7 +462,7 @@
     def pass_detour(off):
         if not detours:
             return
-        for c in (0, 1):
+        for c in BOTH:
 
             @pl.when(edge if c == 0 else edge & (wrap(tor.pos[0] + off, RING) == inner))
             def _():
@@ -474,8 +480,8 @@
     def drain_detours():
         if not detours:
             return
-        for off in (0, -1, 1):
-            for c in (0, 1):
+        for off in (0, -1):
+            for c in BOTH:
 
                 @pl.when(edge if c == 0 else edge & (wrap(tor.pos[0] + off, RING) == inner))
                 def _():
@@ -491,7 +497,6 @@
     g1.spread(1)
     wk_r.step()
     wv_r.step()
-    r_o.start()
     g1.halves(0)
     wq_r.step2()
     wk_r.step2()
@@ -502,18 +507,16 @@
     qkv_group(0)
     g1.relay(1)
     g1.far()
-    r_o.step()
     g1.halves(-1)
     qkv_group(-1)
     g1.halves(1)
     qkv_group(1)
     pass_detour(0)
     g1.relay(2)
-    r_o.step2()
-    pass_detour(-1)
     g1.halves(2)
     qkv_group(2)
-    pass_detour(1)
+    pass_detour(-1)
+    r_o.start()
 
     block = min(seq, 128)
     sends = []
@@ -526,7 +529,7 @@
             def part(which):
                 return x2[pl.ds(s * tx_count, tx_count), :, col(c3 + which * hc + hd * HEAD_DIM, HEAD_DIM)].reshape(seq, HEAD_DIM)
 
-            for which in (0, 1):
+            for which in BOTH:
                 v = part(which).astype(F32)
                 rot = v * cos_ref[...] + pltpu.roll(v, HEAD_DIM // 2, 1) * sin_ref[...]
                 kv[which] = rot.astype(BF16)
@@ -554,6 +557,7 @@
         oe.start()
         sends.append(oe)
 
+    r_o.step()
     g1.drain()
     drain_detours()
     view = x2.at[pl.ds(0, (tx_count - 1) * spd), :, pl.ds(0, c3)]
@@ -561,6 +565,7 @@
     for oe in sends:
         oe.wait()
         oe.drain()
+    r_o.step2()
     r_gate.start(place=False)
     r_up.start(place=False)
     r_down.start()
@@ -606,7 +611,7 @@
     g2.start()
     sc1.drain()
 
-    def mlp_group(off, between):
+    def mlp_group(off, between, mid):
         stage(x2, off, xs, pl.ds(0, d))
         width = 256 if fp % 256 == 0 else 128
 
@@ -618,10 +623,14 @@
             act[:, cols] = (gate * jax.nn.sigmoid(gate) * up).astype(BF16)
 
         between()
-
-        @pl.loop(0, tx_count)
-        def _(x):
-            put(off, x, jnp.dot(act[...], wd[x], preferred_element_type=F32).astype(BF16))
+        half = tx_count // 2
+        for lo, then in ((0, mid), (half, nothing)):
+
+            @pl.loop(lo, lo + half)
+            def _(x):
+                put(off, x, jnp.dot(act[...], wd[x], preferred_element_type=F32).astype(BF16))
+
+            then()
 
     sc2 = Scatter(tor, xp, rs_bufs, (-1, 1, 2, 0))
     g2.near()
@@ -635,22 +644,24 @@
     r_gate.finish(place=False)
     r_up.finish(place=False)
 
-    def rest():
+    def weights_in():
+        r_down.step2()
+        r_down.finish()
+
+    def onward():
         g2.relay(-1)
         g2.far()
-        r_down.step2()
-        r_down.finish()
-
-    mlp_group(0, rest)
+
+    mlp_group(0, weights_in, onward)
     g2.relay(1)
     g2.halves(-1)
-    mlp_group(-1, lambda: g2.relay(2))
+    mlp_group(-1, nothing, lambda: g2.relay(2))
     sc2.issue(0)
     g2.halves(1)
-    mlp_group(1, lambda: None)
+    mlp_group(1, nothing, nothing)
     sc2.issue(1)
     g2.halves(2)
-    mlp_group(2, lambda: None)
+    mlp_group(2, nothing, nothing)
     sc2.issue(2)
     sc2.augment(0)
     sc2.augment(1)

time: 248 us -> 248 us (level)
  no operation moved by 1% of the time
where the time goes in v6:
time: 248 us
  Pallas kernels  246 us (99%)
    pallas_call x1, Pallas kernels, layer_fn(): pl.pallas_call(functools.partial(layer_kernel, tx_count), name='layer', o...  246 us

profile of v6, /device:TPU:1, one launch (start us, length us, event | category | flops | bytes accessed | tf_op | source)
XLA Modules:
  0.0 248.1 jit_solution(5653755098301956545)
XLA Ops:
  0.0 246.3 %layer.1 = bf16[512,512]{1,0:T(8,128)(2,1)} custom-call(bf16[512,512]{1,0:T(8,128)(2,1)} %bitcast.7, bf16[512,256]{1,0:T(8,128)(2,1)} %wq_ref.1, bf16[512,256]{1,0:T(8,128)(2,1)} %wk_ref.1, bf16[512,256]{1,0:T(8,128)(2,1)} %wv_ref.1, bf16[256,512]{1,0:T(8,128)(2,1)} %wo_ref.1, bf16[688,512]{1,0:T(8,128)(2,1)} %bitcast.5, bf16[688,512]{1,0:T(8,128)(2,1)} %bitcast.6, ...), custom_call_target="tpu_custom_call" | custom-call | tf_op jit(solution)/shard_map/layer/pallas_call | solution.py:731
  246.3 1.9 copy.12

commit v7 on v6

--- a/solution.py
+++ b/solution.py
@@ -89,8 +89,14 @@
     def recv(self, c, ph, off, d):
         self.copy(c, ph, off, d, False, 1).wait_recv()
 
+    def far_copy(self, c, d, second, hops):
+        s = self.tor.slot(self.first(c), 2, -d * hops)
+        view = self.buf.at[s, self.rows(c, -d if second else d, True)]
+        i = self.sem(c, 2, 2, d, second)
+        return remote(view, view, self.ssem, self.rsem.at[i], {"ty": self.tor.slot(self.first(c), 0, d)})
+
     def recv_halves(self, ph, off):
-        view = self.buf.at[0]
+        view = self.buf.at[pl.ds(0, 2)] if ph == off == 2 else self.buf.at[0]
         remote(view, view, self.ssem, self.rsem.at[self.sem(0, ph, off, 1, True)], {"ty": self.tor.me}).wait_recv()
 
     def start(self):
@@ -113,12 +119,18 @@
     def relay(self, off):
         for d in DIRS:
             for c in BOTH:
-                self.recv(c, 2, off, d)
+                if off == 2:
+                    self.far_copy(c, d, False, 1).wait_recv()
+                else:
+                    self.recv(c, 2, off, d)
                 self.send(c, 2, off, d, True)
 
-    def far(self):
-        self.recv_halves(1, 0)
-        self.spread(2)
+    def far(self, second):
+        if not second:
+            self.recv_halves(1, 0)
+        for c in BOTH:
+            for d in DIRS:
+                self.far_copy(c, d, second, 0).start()
 
     def halves(self, off):
         self.recv_halves(2, off)
@@ -501,18 +513,19 @@
     wq_r.step2()
     wk_r.step2()
     g1.relay(-1)
+    g1.far(False)
     wv_r.step2()
     for r in rings:
         r.finish()
     qkv_group(0)
     g1.relay(1)
-    g1.far()
+    g1.far(True)
     g1.halves(-1)
     qkv_group(-1)
+    g1.relay(2)
     g1.halves(1)
     qkv_group(1)
     pass_detour(0)
-    g1.relay(2)
     g1.halves(2)
     qkv_group(2)
     pass_detour(-1)
@@ -644,16 +657,15 @@
     r_gate.finish(place=False)
     r_up.finish(place=False)
 
-    def weights_in():
+    def onward():
+        g2.relay(-1)
+        g2.far(False)
         r_down.step2()
         r_down.finish()
 
-    def onward():
-        g2.relay(-1)
-        g2.far()
-
-    mlp_group(0, weights_in, onward)
+    mlp_group(0, onward, nothing)
     g2.relay(1)
+    g2.far(True)
     g2.halves(-1)
     mlp_group(-1, nothing, lambda: g2.relay(2))
     sc2.issue(0)
@@ -725,7 +737,7 @@
             bf(tx_count, dx, fp), bf(tx_count, dx, fp), bf(tx_count, fp, dx),
             bf(rows, d), bf(rows, hc), bf(rows, fp), bf(3, seq, HEAD_DIM), bf(tok, d), bf(tok, d), bf(seq, dx),
             pltpu.VMEM((seq, HEAD_DIM), F32), pltpu.VMEM((seq, HEAD_DIM), F32),
-            dma((5,)), dma((spd + 2,)), dma((spd + 2,)), dma, dma((spd,)), dma, dma((6,)),
+            dma((5,)), dma((spd + 2,)), dma((spd + 2,)), dma, dma((spd,)), dma, dma((4,)),
             dma, dma((Gather.SEMS,)), dma((7,)), dma((7, Ring.SEMS)),
         ] + Scatter.buffers(tok, d)
         y = pl.pallas_call(

time: 248 us -> 239 us (0.964)
  Pallas kernels: 246 us -> 237 us
    pallas_call x1, Pallas kernels: 246 us -> 237 us  [layer_fn(): pl.pallas_call(functools.partial(layer_kernel, tx_count), name='layer', o...]
where the time goes in v7:
time: 239 us
  Pallas kernels  237 us (99%)
    pallas_call x1, Pallas kernels, layer_fn(): pl.pallas_call(functools.partial(layer_kernel, tx_count), name='layer', o...  237 us

profile of v7, /device:TPU:1, one launch (start us, length us, event | category | flops | bytes accessed | tf_op | source)
XLA Modules:
  0.0 238.8 jit_solution(14251764629368958894)
XLA Ops:
  0.0 236.9 %layer.1 = bf16[512,512]{1,0:T(8,128)(2,1)} custom-call(bf16[512,512]{1,0:T(8,128)(2,1)} %bitcast.7, bf16[512,256]{1,0:T(8,128)(2,1)} %wq_ref.1, bf16[512,256]{1,0:T(8,128)(2,1)} %wk_ref.1, bf16[512,256]{1,0:T(8,128)(2,1)} %wv_ref.1, bf16[256,512]{1,0:T(8,128)(2,1)} %wo_ref.1, bf16[688,512]{1,0:T(8,128)(2,1)} %bitcast.5, bf16[688,512]{1,0:T(8,128)(2,1)} %bitcast.6, ...), custom_call_target="tpu_custom_call" | custom-call | tf_op jit(solution)/shard_map/layer/pallas_call | solution.py:743
  236.9 1.9 copy.12

commit v8 on v7

--- a/solution.py
+++ b/solution.py
@@ -447,25 +447,32 @@
             for c, s, at in pieces(off):
                 x2[s, pl.ds(c * q2, q2), cols] = out[at : at + q2]
 
-        for c, s, _ in pieces(off):
-            p, sl = lax.div(s, spd), lax.rem(s, spd)
-            rows = pl.ds(c * q2, q2)
-            src = x2.at[s, rows, pl.ds(0, c3)]
-            dst = x2.at[sl * tx_count + me_tx, rows, pl.ds(c3, c3)]
-
-            detour = (p != p) if off > 0 or not detours else edge & (lax.div(p, 2) == opposite)
-
-            @pl.when(p == me_tx)
-            def _():
-                pltpu.make_async_copy(src, dst, qkv_r.at[sl]).start()
-
-            @pl.when(detour)
-            def _():
-                remote(src, x2.at[s, rows, via], qkv_s, via_r.at[2 * AWAY.index(off) + c], {"tx": over}).start()
-
-            @pl.when((p != me_tx) & jnp.logical_not(detour))
-            def _():
-                remote(src, dst, qkv_s, qkv_r.at[sl], {"tx": p}).start()
+        def hand_out(chosen):
+            for c, s, _ in pieces(off):
+                p, sl = lax.div(s, spd), lax.rem(s, spd)
+                now = chosen(sl)
+                rows = pl.ds(c * q2, q2)
+                src = x2.at[s, rows, pl.ds(0, c3)]
+                dst = x2.at[sl * tx_count + me_tx, rows, pl.ds(c3, c3)]
+                detour = (p != p) if off > 0 or not detours else edge & (lax.div(p, 2) == opposite)
+
+                @pl.when(now & (p == me_tx))
+                def _():
+                    pltpu.make_async_copy(src, dst, qkv_r.at[sl]).start()
+
+                @pl.when(now & detour)
+                def _():
+                    remote(src, x2.at[s, rows, via], qkv_s, via_r.at[2 * AWAY.index(off) + c], {"tx": over}).start()
+
+                @pl.when(now & (p != me_tx) & jnp.logical_not(detour))
+                def _():
+                    remote(src, dst, qkv_s, qkv_r.at[sl], {"tx": p}).start()
+
+        if off == 2:
+            hand_out(lambda sl: sl < spd // 2)
+            hand_out(lambda sl: sl >= spd // 2)
+        else:
+            hand_out(lambda sl: sl >= 0)
 
     def detour_rows(off, c):
         rows = pl.ds(c * q2, q2)
@@ -518,6 +525,7 @@
     for r in rings:
         r.finish()
     qkv_group(0)
+    r_o.start()
     g1.relay(1)
     g1.far(True)
     g1.halves(-1)
@@ -529,7 +537,7 @@
     g1.halves(2)
     qkv_group(2)
     pass_detour(-1)
-    r_o.start()
+    r_o.step()
 
     block = min(seq, 128)
     sends = []
@@ -570,7 +578,6 @@
         oe.start()
         sends.append(oe)
 
-    r_o.step()
     g1.drain()
     drain_detours()
     view = x2.at[pl.ds(0, (tx_count - 1) * spd), :, pl.ds(0, c3)]

time: 239 us -> 241 us (level)
  no operation moved by 1% of the time
where the time goes in v8:
time: 241 us
  Pallas kernels  239 us (99%)
    pallas_call x1, Pallas kernels, layer_fn(): pl.pallas_call(functools.partial(layer_kernel, tx_count), name='layer', o...  239 us

profile of v8, /device:TPU:1, one launch (start us, length us, event | category | flops | bytes accessed | tf_op | source)
XLA Modules:
  0.0 240.6 jit_solution(6038493233861979040)
XLA Ops:
  0.0 238.7 %layer.1 = bf16[512,512]{1,0:T(8,128)(2,1)} custom-call(bf16[512,512]{1,0:T(8,128)(2,1)} %bitcast.7, bf16[512,256]{1,0:T(8,128)(2,1)} %wq_ref.1, bf16[512,256]{1,0:T(8,128)(2,1)} %wk_ref.1, bf16[512,256]{1,0:T(8,128)(2,1)} %wv_ref.1, bf16[256,512]{1,0:T(8,128)(2,1)} %wo_ref.1, bf16[688,512]{1,0:T(8,128)(2,1)} %bitcast.5, bf16[688,512]{1,0:T(8,128)(2,1)} %bitcast.6, ...), custom_call_target="tpu_custom_call" | custom-call | tf_op jit(solution)/shard_map/layer/pallas_call | solution.py:750
  238.7 1.9 copy.12

commit v9 on v8

--- a/solution.py
+++ b/solution.py
@@ -525,7 +525,6 @@
     for r in rings:
         r.finish()
     qkv_group(0)
-    r_o.start()
     g1.relay(1)
     g1.far(True)
     g1.halves(-1)
@@ -537,7 +536,7 @@
     g1.halves(2)
     qkv_group(2)
     pass_detour(-1)
-    r_o.step()
+    r_o.start()
 
     block = min(seq, 128)
     sends = []
@@ -578,6 +577,7 @@
         oe.start()
         sends.append(oe)
 
+    r_o.step()
     g1.drain()
     drain_detours()
     view = x2.at[pl.ds(0, (tx_count - 1) * spd), :, pl.ds(0, c3)]

time: 241 us -> 239 us (level)
  no operation moved by 1% of the time
where the time goes in v9:
time: 239 us
  Pallas kernels  237 us (99%)
    pallas_call x1, Pallas kernels, layer_fn(): pl.pallas_call(functools.partial(layer_kernel, tx_count), name='layer', o...  237 us

profile of v9, /device:TPU:1, one launch (start us, length us, event | category | flops | bytes accessed | tf_op | source)
XLA Modules:
  0.0 238.8 jit_solution(17022007590857694238)
XLA Ops:
  0.0 236.9 %layer.1 = bf16[512,512]{1,0:T(8,128)(2,1)} custom-call(bf16[512,512]{1,0:T(8,128)(2,1)} %bitcast.7, bf16[512,256]{1,0:T(8,128)(2,1)} %wq_ref.1, bf16[512,256]{1,0:T(8,128)(2,1)} %wk_ref.1, bf16[512,256]{1,0:T(8,128)(2,1)} %wv_ref.1, bf16[256,512]{1,0:T(8,128)(2,1)} %wo_ref.1, bf16[688,512]{1,0:T(8,128)(2,1)} %bitcast.5, bf16[688,512]{1,0:T(8,128)(2,1)} %bitcast.6, ...), custom_call_target="tpu_custom_call" | custom-call | tf_op jit(solution)/shard_map/layer/pallas_call | solution.py:750
  237.0 1.9 copy.12

commit v10 on v9

--- a/solution.py
+++ b/solution.py
@@ -544,29 +544,28 @@
         view = x2.at[pl.ds(s * tx_count, tx_count), :, pl.ds(c3, c3)]
         remote(view, view, qkv_s, qkv_r.at[s], {"tx": me_tx}).wait_recv()
 
-        @pl.loop(0, heads)
-        def _(hd):
-            def part(which):
-                return x2[pl.ds(s * tx_count, tx_count), :, col(c3 + which * hc + hd * HEAD_DIM, HEAD_DIM)].reshape(seq, HEAD_DIM)
+        for hd in range(heads):
+            def part(which, s=s, hd=hd):
+                return x2[pl.ds(s * tx_count, tx_count), :, pl.ds(c3 + which * hc + hd * HEAD_DIM, HEAD_DIM)].reshape(seq, HEAD_DIM)
 
             for which in BOTH:
                 v = part(which).astype(F32)
                 rot = v * cos_ref[...] + pltpu.roll(v, HEAD_DIM // 2, 1) * sin_ref[...]
-                kv[which] = rot.astype(BF16)
-            kv[2] = part(2)
+                kv[hd, which] = rot.astype(BF16)
+            kv[hd, 2] = part(2)
             for b in range(seq // block):
                 keys = (b + 1) * block
-                sc = lax.dot_general(kv[0, pl.ds(b * block, block)], kv[1, pl.ds(0, keys)], (((1,), (1,)), ((), ())), preferred_element_type=F32)
+                sc = lax.dot_general(kv[hd, 0, pl.ds(b * block, block)], kv[hd, 1, pl.ds(0, keys)], (((1,), (1,)), ((), ())), preferred_element_type=F32)
                 sc = sc * HEAD_DIM ** -0.5
                 q_pos = b * block + lax.broadcasted_iota(jnp.int32, (block, keys), 0)
                 k_pos = lax.broadcasted_iota(jnp.int32, (block, keys), 1)
                 sc = jnp.where(q_pos >= k_pos, sc, -1e30)
                 e = jnp.exp(sc - jnp.max(sc, axis=-1, keepdims=True))
                 prob = (e / jnp.sum(e, axis=-1, keepdims=True)).astype(BF16)
-                o = jnp.dot(prob, kv[2, pl.ds(0, keys)], preferred_element_type=F32).astype(BF16)
+                o = jnp.dot(prob, kv[hd, 2, pl.ds(0, keys)], preferred_element_type=F32).astype(BF16)
                 for n in range(block // tok):
                     at = (b * (block // tok) + n) * spd + s
-                    x2[at, :, col(2 * c3 + hd * HEAD_DIM, HEAD_DIM)] = o[n * tok : (n + 1) * tok]
+                    x2[at, :, pl.ds(2 * c3 + hd * HEAD_DIM, HEAD_DIM)] = o[n * tok : (n + 1) * tok]
 
         oe = exchange(
             1 + s,
@@ -742,7 +741,7 @@
         scratch = [
             bf(n_dev, tok, d), bf(n_dev, tok, d), bf(tx_count, dx, 3 * hc), bf(tx_count, hc, dx),
             bf(tx_count, dx, fp), bf(tx_count, dx, fp), bf(tx_count, fp, dx),
-            bf(rows, d), bf(rows, hc), bf(rows, fp), bf(3, seq, HEAD_DIM), bf(tok, d), bf(tok, d), bf(seq, dx),
+            bf(rows, d), bf(rows, hc), bf(rows, fp), bf(hc // HEAD_DIM, 3, seq, HEAD_DIM), bf(tok, d), bf(tok, d), bf(seq, dx),
             pltpu.VMEM((seq, HEAD_DIM), F32), pltpu.VMEM((seq, HEAD_DIM), F32),
             dma((5,)), dma((spd + 2,)), dma((spd + 2,)), dma, dma((spd,)), dma, dma((4,)),
             dma, dma((Gather.SEMS,)), dma((7,)), dma((7, Ring.SEMS)),

time: 239 us -> 239 us (level)
  no operation moved by 1% of the time
where the time goes in v10:
time: 239 us
  Pallas kernels  237 us (99%)
    pallas_call x1, Pallas kernels, layer_fn(): pl.pallas_call(functools.partial(layer_kernel, tx_count), name='layer', o...  237 us

profile of v10, /device:TPU:1, one launch (start us, length us, event | category | flops | bytes accessed | tf_op | source)
XLA Modules:
  0.0 239.0 jit_solution(7921306381571995569)
XLA Ops:
  0.0 237.1 %layer.1 = bf16[512,512]{1,0:T(8,128)(2,1)} custom-call(bf16[512,512]{1,0:T(8,128)(2,1)} %bitcast.7, bf16[512,256]{1,0:T(8,128)(2,1)} %wq_ref.1, bf16[512,256]{1,0:T(8,128)(2,1)} %wk_ref.1, bf16[512,256]{1,0:T(8,128)(2,1)} %wv_ref.1, bf16[256,512]{1,0:T(8,128)(2,1)} %wo_ref.1, bf16[688,512]{1,0:T(8,128)(2,1)} %bitcast.5, bf16[688,512]{1,0:T(8,128)(2,1)} %bitcast.6, ...), custom_call_target="tpu_custom_call" | custom-call | tf_op jit(solution)/shard_map/layer/pallas_call | solution.py:749
  237.1 1.9 copy.12

commit v11 on v7

--- a/solution.py
+++ b/solution.py
@@ -429,7 +429,7 @@
         for c, s, at in pieces(off):
             dst[pl.ds(at, q2), :] = src[s, pl.ds(c * q2, q2), cols]
 
-    detours = tx_count == 8
+    detours = False
     x_pos = lax.div(me_tx, 2)
     edge = (x_pos == 0) | (x_pos == 3)
     opposite = jnp.where(x_pos == 0, 2, 1)

time: 239 us -> 238 us (level)
  no operation moved by 1% of the time
where the time goes in v11:
time: 238 us
  Pallas kernels  236 us (99%)
    pallas_call x1, Pallas kernels, layer_fn(): pl.pallas_call(functools.partial(layer_kernel, tx_count), name='layer', o...  236 us

profile of v11, /device:TPU:1, one launch (start us, length us, event | category | flops | bytes accessed | tf_op | source)
XLA Modules:
  0.0 237.9 jit_solution(8230133293576143030)
XLA Ops:
  0.0 236.0 %layer.1 = bf16[512,512]{1,0:T(8,128)(2,1)} custom-call(bf16[512,512]{1,0:T(8,128)(2,1)} %bitcast.7, bf16[512,256]{1,0:T(8,128)(2,1)} %wq_ref.1, bf16[512,256]{1,0:T(8,128)(2,1)} %wk_ref.1, bf16[512,256]{1,0:T(8,128)(2,1)} %wv_ref.1, bf16[256,512]{1,0:T(8,128)(2,1)} %wo_ref.1, bf16[688,512]{1,0:T(8,128)(2,1)} %bitcast.5, bf16[688,512]{1,0:T(8,128)(2,1)} %bitcast.6, ...), custom_call_target="tpu_custom_call" | custom-call | tf_op jit(solution)/shard_map/layer/pallas_call | solution.py:743
  236.0 1.9 copy.12
